TPU v7x, 32 devices: a whole 2x2x4 slice. The times are simulated.
32 devices in a mesh: dp: 2 (over x), sp: 4 (over z), uly: 4 (over y, core).
Axes of the slice: x: 2, y: 2, z: 4, core: 2. Of those that a mesh axis runs over, the one named last changes fastest.
Arguments:
- tokens: bfloat16 [2, 4608, 5120], P('dp', ('sp', 'uly')), parts along dimension 0
- rope_ang: float32 [4608, 64], P(('sp', 'uly'))
- t_emb: float32 [2, 6, 5120], P('dp'), parts along dimension 0
- block_mod: float32 [1, 6, 5120], replicated
- context: bfloat16 [2, 512, 5120], P('dp'), parts along dimension 0
- attn_wq: bfloat16 [5120, 5120], replicated
- attn_bq: bfloat16 [5120], replicated
- attn_wk: bfloat16 [5120, 5120], replicated
- attn_bk: bfloat16 [5120], replicated
- attn_wv: bfloat16 [5120, 5120], replicated
- attn_bv: bfloat16 [5120], replicated
- attn_gq: bfloat16 [5120], replicated
- attn_gk: bfloat16 [5120], replicated
- attn_wo: bfloat16 [5120, 5120], replicated
- attn_bo: bfloat16 [5120], replicated
- norm3_w: bfloat16 [5120], replicated
- norm3_b: bfloat16 [5120], replicated
- cross_wq: bfloat16 [5120, 5120], replicated
- cross_wk: bfloat16 [5120, 5120], replicated
- cross_wv: bfloat16 [5120, 5120], replicated
- cross_gq: bfloat16 [5120], replicated
- cross_gk: bfloat16 [5120], replicated
- cross_wo: bfloat16 [5120, 5120], replicated
- ffn_w1: bfloat16 [5120, 13824], replicated
- ffn_w2: bfloat16 [13824, 5120], replicated
Outputs:
- output: bfloat16 [2, 4608, 5120], P('dp', ('sp', 'uly')), parts along dimension 0
There are 2 independent parts. A program takes and returns all parts, laid end to end along the dimension named above; an argument that names none is the same for every part.
All inputs are finite; a program needn't handle non-finite values.
Results may differ from a plain program's by a relative error of at most 0.00568233.
Values are sent between devices in bfloat16 or wider.
A program may use at most 2.75 GiB of HBM per device.

v0:
```python
import jax
import jax.numpy as jnp
from jax import lax
from jax.sharding import PartitionSpec as P, NamedSharding

EPS = 1e-6
HEAD = 128


def layer_norm(x_f32):
    mean_x = jnp.mean(x_f32, axis=-1, keepdims=True)
    centered = x_f32 - mean_x
    var_x = jnp.mean(centered * centered, axis=-1, keepdims=True)
    return centered * lax.rsqrt(var_x + EPS)


def rms_norm(h_lin, gain):
    return h_lin * lax.rsqrt(jnp.mean(h_lin * h_lin, axis=-1, keepdims=True) + EPS) * gain.astype(jnp.float32)


def apply_rope(heads, cos_ang, sin_ang):
    pairs = heads.reshape(heads.shape[:-1] + (HEAD // 2, 2))
    pair_a = pairs[..., 0]
    pair_b = pairs[..., 1]
    turned = jnp.stack([pair_a * cos_ang - pair_b * sin_ang, pair_a * sin_ang + pair_b * cos_ang], axis=-1)
    return turned.reshape(heads.shape)


def project(operand, weight):
    return jnp.dot(operand, weight, preferred_element_type=jnp.float32)


def attention(q_b, k_b, v_b):
    scores = jnp.einsum('bqhd,bkhd->bhqk', q_b, k_b, preferred_element_type=jnp.float32) * (HEAD ** -0.5)
    weights = jnp.exp(scores - jnp.max(scores, axis=-1, keepdims=True))
    weight_sum = jnp.sum(weights, axis=-1)
    weighted_v = jnp.einsum('bhqk,bkhd->bqhd', weights.astype(jnp.bfloat16), v_b, preferred_element_type=jnp.float32)
    return (weighted_v / jnp.transpose(weight_sum, (0, 2, 1))[..., None]).astype(jnp.bfloat16)


def self_qkv(tokens, rope_ang, ada_mod, attn_wq, attn_bq, attn_wk, attn_bk, attn_wv, attn_bv, attn_gq, attn_gk):
    n_batch, n_tok, width = tokens.shape
    head_shape = (n_batch, n_tok, width // HEAD, HEAD)
    x_res = tokens.astype(jnp.float32)
    y_mod = (layer_norm(x_res) * (1.0 + ada_mod[:, 1:2]) + ada_mod[:, 0:1]).astype(jnp.bfloat16)
    cos_ang = jnp.cos(rope_ang)[:, None, :]
    sin_ang = jnp.sin(rope_ang)[:, None, :]
    q_tok = apply_rope(rms_norm(project(y_mod, attn_wq) + attn_bq.astype(jnp.float32), attn_gq).reshape(head_shape), cos_ang, sin_ang).astype(jnp.bfloat16)
    k_tok = apply_rope(rms_norm(project(y_mod, attn_wk) + attn_bk.astype(jnp.float32), attn_gk).reshape(head_shape), cos_ang, sin_ang).astype(jnp.bfloat16)
    v_tok = (project(y_mod, attn_wv) + attn_bv.astype(jnp.float32)).astype(jnp.bfloat16).reshape(head_shape)
    return x_res, q_tok, k_tok, v_tok


def block_tail(x_res, attn_heads, context, ada_mod, attn_wo, attn_bo, norm3_w, norm3_b, cross_wq, cross_wk, cross_wv, cross_gq, cross_gk, cross_wo, ffn_w1, ffn_w2):
    n_batch, n_tok, width = x_res.shape
    n_heads = width // HEAD
    n_text = context.shape[1]
    attn_out = attn_heads.reshape(n_batch, n_tok, width)
    x_one = x_res + ada_mod[:, 2:3] * (project(attn_out, attn_wo) + attn_bo.astype(jnp.float32))
    z_norm = (layer_norm(x_one) * norm3_w.astype(jnp.float32) + norm3_b.astype(jnp.float32)).astype(jnp.bfloat16)
    cross_q = rms_norm(project(z_norm, cross_wq), cross_gq).astype(jnp.bfloat16).reshape(n_batch, n_tok, n_heads, HEAD)
    cross_k = rms_norm(project(context, cross_wk), cross_gk).astype(jnp.bfloat16).reshape(n_batch, n_text, n_heads, HEAD)
    cross_v = project(context, cross_wv).astype(jnp.bfloat16).reshape(n_batch, n_text, n_heads, HEAD)
    cross_out = attention(cross_q, cross_k, cross_v).reshape(n_batch, n_tok, width)
    x_two = x_one + project(cross_out, cross_wo)
    hidden = (layer_norm(x_two) * (1.0 + ada_mod[:, 4:5]) + ada_mod[:, 3:4]).astype(jnp.bfloat16)
    gelu_out = jax.nn.gelu(project(hidden, ffn_w1), approximate=True).astype(jnp.bfloat16)
    return (x_two + ada_mod[:, 5:6] * project(gelu_out, ffn_w2)).astype(jnp.bfloat16)


def solution(mesh):
    tok_spec = P('dp', ('sp', 'uly'), None)
    batch_spec = P('dp', None, None)

    def local_block(tokens, rope_ang, t_emb, block_mod, context, attn_wq, attn_bq, attn_wk, attn_bk, attn_wv, attn_bv, attn_gq, attn_gk, attn_wo, attn_bo, norm3_w, norm3_b, cross_wq, cross_wk, cross_wv, cross_gq, cross_gk, cross_wo, ffn_w1, ffn_w2):
        ada_mod = t_emb + block_mod
        x_res, q_tok, k_tok, v_tok = self_qkv(tokens, rope_ang, ada_mod, attn_wq, attn_bq, attn_wk, attn_bk, attn_wv, attn_bv, attn_gq, attn_gk)
        q_head = lax.all_to_all(q_tok, 'uly', 2, 1, tiled=True)
        k_head = lax.all_to_all(k_tok, 'uly', 2, 1, tiled=True)
        v_head = lax.all_to_all(v_tok, 'uly', 2, 1, tiled=True)
        k_all = lax.all_gather(k_head, 'sp', axis=1, tiled=True)
        v_all = lax.all_gather(v_head, 'sp', axis=1, tiled=True)
        o_head = attention(q_head, k_all, v_all)
        o_tok = lax.all_to_all(o_head, 'uly', 1, 2, tiled=True)
        return block_tail(x_res, o_tok, context, ada_mod, attn_wo, attn_bo, norm3_w, norm3_b, cross_wq, cross_wk, cross_wv, cross_gq, cross_gk, cross_wo, ffn_w1, ffn_w2)

    in_specs = (tok_spec, P(('sp', 'uly'), None), batch_spec, P(), batch_spec) + (P(),) * 20
    return jax.shard_map(local_block, mesh=mesh, in_specs=in_specs, out_specs=tok_spec, check_vma=False)
```

profile of v0, /device:TPU:8, one launch (start us, length us, event | category | flops | bytes accessed | tf_op | source)
XLA Modules:
  0.0 1014.7 jit_solution(336606250758218684)
XLA Ops:
  13.6 25.5 %multiply_reduce_fusion.6 = (f32[288]{0:T(512)S(1)}, f32[288,5120]{1,0:T(8,128)}) fusion(f32[5120]{0:T(1024)S(1)} %convert_element_type.107, bf16[5120,5120]{1,0:T(8,128)(2,1)} %param.30, bf16[1,288,5120]{2,1,0:T(8,128)(2,1)S(1)} %copy-done, f32[5120]{0:T(1024)S(1)} %bitcast.169, f32[5120]{0:T(1024)S(1)} %bitcast.172, f32[288]{0:T(512)S(1)} %add_rsqrt_fusion.6, ...), kind=kOutput, calls=%fused_computation.67 | convolution fusion | flops 15112765440 | bytes 61341056 | tf_op jit(solution)/shard_map/dot_general | solution.py:30
  53.5 9.9 reshape_reshape.6
  63.5 25.5 %multiply_reduce_fusion.5 = (f32[288]{0:T(512)S(1)}, f32[288,5120]{1,0:T(8,128)}) fusion(f32[5120]{0:T(1024)S(1)} %convert_element_type.110, bf16[5120,5120]{1,0:T(8,128)(2,1)} %param.32, bf16[1,288,5120]{2,1,0:T(8,128)(2,1)S(1)} %copy-done, f32[5120]{0:T(1024)S(1)} %bitcast.170, f32[5120]{0:T(1024)S(1)} %bitcast.173, f32[288]{0:T(512)S(1)} %add_rsqrt_fusion.6, ...), kind=kOutput, calls=%fused_computation.65 | convolution fusion | flops 15112765440 | bytes 61341056 | tf_op jit(solution)/shard_map/dot_general | solution.py:30
  103.3 10.0 reshape_reshape.7
  113.7 23.4 %subtract_convert_fusion = (bf16[1,288,40,64,1]{1,4,3,2,0:T(2,128)(2,1)S(1)}, bf16[1,288,40,64,1]{1,4,3,2,0:T(2,128)(2,1)S(1)}, bf16[1,288,40,64,1]{1,4,3,2,0:T(2,128)(2,1)S(1)}, bf16[1,288,40,64,1]{1,4,3,2,0:T(2,128)(2,1)S(1)}) fusion(f32[1,288,40,64,2]{1,4,3,2,0:T(2,128)} %reshape_reshape.7, f32[288,64]{0,1:T(8,128)S(1)} %get-tuple-element.18, ...), kind=kLoop, calls=%fused_computation.80 | loop fusion | flops 11796480 | bytes 17842176 | tf_op jit(solution)/shard_map/convert
  137.1 19.8 %pad_maximum_fusion = (bf16[1,288,40,64,2]{1,4,3,2,0:T(2,128)(2,1)}, bf16[1,288,40,64,2]{1,4,3,2,0:T(2,128)(2,1)S(1)}) fusion(bf16[1,288,40,64,1]{1,4,3,2,0:T(2,128)(2,1)S(1)} %get-tuple-element.9, bf16[1,288,40,64,1]{1,4,3,2,0:T(2,128)(2,1)S(1)} %get-tuple-element.10, bf16[1,288,40,64,1]{1,4,3,2,0:T(2,128)(2,1)S(1)} %get-tuple-element.6, ...), kind=kLoop, calls=%fused_computation.77 | loop fusion | flops 11796480 | bytes 11796480 | tf_op jit(solution)/shard_map/stack | solution.py:25
  169.0 38.4 %all_to_all.66 = bf16[1,288,40,128]{3,1,0,2:T(8,128)(2,1)S(1)} all-to-all(bf16[1,288,40,128]{3,1,0,2:T(8,128)(2,1)} %copy.58), channel_id=1, replica_groups=mesh['dp'=2,'sp'=4,'uly'=4] {'uly'}, dimensions={2} | all-to-all | bytes 5898240 | tf_op jit(solution)/shard_map/all_to_all | solution.py:79
  228.3 24.2 %fusion.87 = bf16[36,8,40,128]{3,1,2,0:T(8,128)(2,1)} fusion(f32[5120]{0:T(1024)S(1)} %convert_element_type.105, bf16[5120,5120]{1,0:T(8,128)(2,1)} %param.34, bf16[1,288,5120]{2,1,0:T(8,128)(2,1)S(1)} %copy-done, f32[5120]{0:T(1024)S(1)} %bitcast.171, f32[5120]{0:T(1024)S(1)} %bitcast.174, f32[288]{0:T(512)S(1)} %add_rsqrt_fusion.6, ...), kind=kOutput, calls=%fused_computation.102 | convolution fusion | flops 15111290880 | bytes 58390784 | tf_op jit(solution)/shard_map/dot_general | solution.py:30
  267.5 35.9 %multiply_reduce_fusion.1 = (f32[512]{0:T(512)}, f32[512,5120]{1,0:T(8,128)}) fusion(bf16[5120,5120]{1,0:T(8,128)(2,1)} %param.43, bf16[1,512,5120]{2,1,0:T(8,128)(2,1)} %param.29), kind=kOutput, calls=%fused_computation.25 | convolution fusion | flops 26848788480 | bytes 68159488 | tf_op jit(solution)/shard_map/dot_general | solution.py:30
  314.7 97.7 %all-gather.5.cloned.1.call-done = bf16[1,4608,10,128]{3,1,2,0:T(8,128)(2,1)} async-done(((bf16[1,1152,10,128]{3,1,2,0:T(8,128)(2,1)}), bf16[1,4608,10,128]{3,1,2,0:T(8,128)(2,1)}) %all-gather.5.cloned.1.call-update) | async-done | bytes 11796496 | tf_op jit(solution)/shard_map/all_gather | solution.py:81
  412.4 72.5 %fusion.102 = (f32[10,1152]{1,0:T(8,128)S(1)}, f32[10,1152,4608]{2,1,0:T(8,128)}) fusion(bf16[1152,10,128]{2,0,1:T(8,128)(2,1)S(1)} %bitcast.153, bf16[1,4608,10,128]{3,1,2,0:T(8,128)(2,1)} %all-gather.5.cloned.1.call-done), kind=kOutput, calls=%fused_computation.122 | convolution fusion | flops 13695702016 | bytes 227128320 | tf_op jit(solution)/shard_map/bqhd,bkhd->bhqk/dot_general | solution.py:34
  484.9 64.1 %fusion = f32[10,1152]{1,0:T(8,128)S(1)} fusion(f32[10,1152,4608]{2,1,0:T(8,128)} %get-tuple-element.24, f32[10,1152]{1,0:T(8,128)S(1)} %get-tuple-element.23), kind=kLoop, calls=%fused_computation.2 | loop fusion | flops 106156800 | bytes 212428800 | tf_op jit(solution)/shard_map/reduce_sum | solution.py:36
  549.0 68.9 %all-gather.3.cloned.1.call-done = bf16[1,4608,10,128]{1,3,2,0:T(8,128)(2,1)} async-done(((bf16[1,1152,10,128]{1,3,2,0:T(8,128)(2,1)}), bf16[1,4608,10,128]{1,3,2,0:T(8,128)(2,1)}) %all-gather.3.cloned.1.call-update) | async-done | bytes 11796496 | tf_op jit(solution)/shard_map/all_gather | solution.py:82
  618.0 69.2 %fusion.50 = bf16[1,1152,10,128]{1,3,2,0:T(8,128)(2,1)S(1)} fusion(f32[10,1152,4608]{2,1,0:T(8,128)} %get-tuple-element.24, f32[10,1152]{1,0:T(8,128)S(1)} %get-tuple-element.23, bf16[1,4608,10,128]{1,3,2,0:T(8,128)(2,1)} %all-gather.3.cloned.1.call-done, f32[1152,10]{0,1:T(8,128)S(1)} %bitcast.163), kind=kOutput, calls=%fused_computation.57 | convolution fusion | flops 13698662400 | bytes 227174400 | tf_op jit(solution)/shard_map/bhqk,bkhd->bqhd/dot_general | solution.py:37
  698.3 35.2 %fusion.84 = bf16[64,40,8,128]{3,2,1,0:T(8,128)(2,1)} fusion(bf16[5120,5120]{1,0:T(8,128)(2,1)} %param.44, bf16[1,512,5120]{2,1,0:T(8,128)(2,1)} %param.29), kind=kOutput, calls=%fused_computation.101 | convolution fusion | flops 26846167040 | bytes 62914560 | tf_op jit(solution)/shard_map/dot_general | solution.py:30
  733.6 18.1 %all-to-all-done.3 = bf16[1,1152,10,128]{3,2,0,1:T(8,128)(2,1)} async-done(((bf16[1,1152,10,128]{3,2,0,1:T(8,128)(2,1)}), bf16[1,1152,10,128]{3,2,0,1:T(8,128)(2,1)}, u32[]{:S(2)}, u32[]{:S(2)}) %all-to-all-start.3) | async-done | bytes 2949152 | tf_op jit(solution)/shard_map/all_to_all | solution.py:84
  762.1 26.8 %fusion.103 = (f32[288]{0:T(512)S(1)}, f32[1,288,5120]{2,1,0:T(8,128)}) fusion(f32[5120]{0:T(1024)S(1)} %convert_element_type.115, bf16[288,5120]{0,1:T(8,128)(2,1)} %bitcast.161, bf16[5120,5120]{1,0:T(8,128)(2,1)} %param.38, f32[5120]{0:T(1024)S(1)} %bitcast.168, bf16[1,288,5120]{2,1,0:T(8,128)(2,1)S(1)} %copy-done.1), kind=kOutput, calls=%fused_computation.123 | convolution fusion | flops 15106867200 | bytes 64267392 | tf_op jit(solution)/shard_map/dot_general | solution.py:30
  792.4 27.4 %multiply_reduce_fusion.3 = (f32[288]{0:T(512)S(1)}, f32[288,5120]{1,0:T(8,128)}) fusion(bf16[5120,5120]{1,0:T(8,128)(2,1)} %param.42, f32[1,288,5120]{2,1,0:T(8,128)} %get-tuple-element.28, f32[5120]{0:T(1024)S(1)} %convert_element_type.118, f32[5120]{0:T(1024)S(1)} %convert_element_type.117, f32[288]{0:T(512)S(1)} %add_rsqrt_fusion.3, ...), kind=kOutput, calls=%fused_computation.61 | convolution fusion | flops 15109816320 | bytes 64269696 | tf_op jit(solution)/shard_map/dot_general | solution.py:30
  819.8 14.8 %multiply_reduce_fusion = (f32[40,288]{1,0:T(8,128)S(1)}, f32[40,288,512]{2,1,0:T(8,128)}) fusion(f32[512,5120]{1,0:T(8,128)} %get-tuple-element.26, f32[5120]{0:T(1024)S(1)} %convert_element_type.122, f32[512]{0:T(512)S(1)} %add_rsqrt_fusion.1, f32[288,5120]{1,0:T(8,128)} %get-tuple-element.30, f32[5120]{0:T(1024)S(1)} %convert_element_type.120, ...), kind=kOutput, calls=%fused_computation.8 | convolution fusion | flops 1534022400 | bytes 40067200 | tf_op jit(solution)/shard_map/bqhd,bkhd->bhqk/dot_general | solution.py:34
  834.5 11.2 %fusion.5 = f32[40,288]{1,0:T(8,128)S(1)} fusion(f32[40,288,512]{2,1,0:T(8,128)} %get-tuple-element.32, f32[40,288]{1,0:T(8,128)S(1)} %get-tuple-element.31), kind=kLoop, calls=%fused_computation.9 | loop fusion | flops 17683200 | bytes 23685120 | tf_op jit(solution)/shard_map/reduce_sum | solution.py:36
  845.7 12.2 %fusion.49 = bf16[1,288,40,128]{3,1,2,0:T(8,128)(2,1)S(1)} fusion(f32[288,40]{0,1:T(8,128)S(1)} %bitcast.164, bf16[64,40,8,128]{3,2,1,0:T(8,128)(2,1)} %fusion.84, f32[40,288,512]{2,1,0:T(8,128)} %get-tuple-element.32, f32[40,288]{1,0:T(8,128)S(1)} %get-tuple-element.31), kind=kOutput, calls=%fused_computation.55 | convolution fusion | flops 1530593280 | bytes 31877120 | tf_op jit(solution)/shard_map/bhqk,bkhd->bqhd/dot_general | solution.py:37
  859.0 26.5 %fusion.104 = (f32[288]{0:T(512)S(1)}, f32[1,288,5120]{2,1,0:T(8,128)}) fusion(f32[1,288,5120]{2,1,0:T(8,128)} %get-tuple-element.28, bf16[5120,5120]{1,0:T(8,128)(2,1)} %param.47, bf16[36,8,40,128]{3,2,1,0:T(8,128)(2,1)S(1)} %bitcast.162), kind=kOutput, calls=%fused_computation.124 | convolution fusion | flops 15102443520 | bytes 67175552 | tf_op jit(solution)/shard_map/dot_general | solution.py:30
  889.0 59.3 %fusion.69 = f32[288,13824]{1,0:T(8,128)} fusion(bf16[5120,13824]{1,0:T(8,128)(2,1)} %param.48, f32[1,288,5120]{2,1,0:T(8,128)} %get-tuple-element.34, f32[5120]{0:T(1024)S(1)} %bitcast.166, f32[5120]{0:T(1024)S(1)} %bitcast.167, f32[288]{0:T(512)S(1)} %add_rsqrt_fusion, f32[288]{0:T(512)S(1)} %broadcast_multiply_fusion), kind=kOutput, calls=%fused_computation.87 | convolution fusion | flops 40776007680 | bytes 163424512 | tf_op jit(solution)/shard_map/dot_general | solution.py:30
  948.3 59.1 %fusion.41 = bf16[1,288,5120]{2,1,0:T(8,128)(2,1)} fusion(f32[1,288,5120]{2,1,0:T(8,128)} %get-tuple-element.34, bf16[13824,5120]{1,0:T(8,128)(2,1)} %param.49, f32[288,13824]{1,0:T(8,128)} %fusion.69, f32[5120]{0:T(1024)S(1)} %bitcast.165), kind=kOutput, calls=%fused_computation.48 | convolution fusion | flops 40808890368 | bytes 166350848 | tf_op jit(solution)/shard_map/dot_general | solution.py:30
  (90 shorter events, 125.0 us)
Async XLA Ops:
  6.5 7.1 copy-start
  6.5 7.0 copy-start.7
  6.5 405.9 %all-gather.5.cloned.1.call-start = ((), (), s32[]{:S(2)}) async-start(), calls=%async_computation.5 | async-start | bytes 14745600 | tf_op jit(solution)/shard_map/all_gather | solution.py:81
  13.6 25.6 %copy-start.8 = (bf16[5120]{0:T(1024)(128)(2,1)S(1)}, bf16[5120]{0:T(1024)(128)(2,1)}, u32[]{:S(2)}) copy-start(bf16[5120]{0:T(1024)(128)(2,1)} %param.36) | copy-start | bytes 30724
  53.5 9.9 copy-start.9
  63.4 25.5 %copy-start.10 = (bf16[5120]{0:T(1024)(128)(2,1)S(1)}, bf16[5120]{0:T(1024)(128)(2,1)}, u32[]{:S(2)}) copy-start(bf16[5120]{0:T(1024)(128)(2,1)} %param.37) | copy-start | bytes 30724
  103.3 10.0 copy-start.2
  217.7 10.6 %copy-start.11 = (bf16[5120]{0:T(1024)(128)(2,1)S(1)}, bf16[5120]{0:T(1024)(128)(2,1)}, u32[]{:S(2)}) copy-start(bf16[5120]{0:T(1024)(128)(2,1)} %param.35) | copy-start | bytes 30724
  223.7 39.2 %all-to-all-start.1 = ((bf16[1,288,40,128]{3,1,0,2:T(8,128)(2,1)}), bf16[1,288,40,128]{3,1,0,2:T(8,128)(2,1)}, u32[]{:S(2)}, u32[]{:S(2)}) async-start(bf16[1,288,40,128]{3,1,0,2:T(8,128)(2,1)} %copy.54), calls=%async_computation.1 | async-start | bytes 5898240 | tf_op jit(solution)/shard_map/all_to_all | solution.py:78
  262.8 42.7 %all-to-all-start = ((bf16[1,288,40,128]{3,1,0,2:T(8,128)(2,1)}), bf16[1,288,40,128]{3,1,0,2:T(8,128)(2,1)}, u32[]{:S(2)}, u32[]{:S(2)}) async-start(bf16[1,288,40,128]{3,1,0,2:T(8,128)(2,1)} %copy.49), calls=%async_computation | async-start | bytes 5898240 | tf_op jit(solution)/shard_map/all_to_all | solution.py:80
  267.4 350.5 %all-gather.3.cloned.1.call-start = ((), (), s32[]{:S(2)}) async-start(), calls=%async_computation.4 | async-start | bytes 14745600 | tf_op jit(solution)/shard_map/all_gather | solution.py:82
  692.9 58.8 %all-to-all-start.3 = ((bf16[1,1152,10,128]{3,2,0,1:T(8,128)(2,1)}), bf16[1,1152,10,128]{3,2,0,1:T(8,128)(2,1)}, u32[]{:S(2)}, u32[]{:S(2)}) async-start(bf16[1,1152,10,128]{3,2,0,1:T(8,128)(2,1)} %copy.60), calls=%async_computation.3 | async-start | bytes 9437184 | tf_op jit(solution)/shard_map/all_to_all | solution.py:84
  698.2 35.3 %copy-start.12 = (bf16[5120]{0:T(1024)(128)(2,1)S(1)}, bf16[5120]{0:T(1024)(128)(2,1)}, u32[]{:S(2)}) copy-start(bf16[5120]{0:T(1024)(128)(2,1)} %param.39) | copy-start | bytes 30724
  698.3 35.3 %copy-start.13 = (bf16[5120]{0:T(1024)(128)(2,1)S(1)}, bf16[5120]{0:T(1024)(128)(2,1)}, u32[]{:S(2)}) copy-start(bf16[5120]{0:T(1024)(128)(2,1)} %param.40) | copy-start | bytes 30724
  698.3 35.3 %copy-start.14 = (bf16[5120]{0:T(1024)(128)(2,1)S(1)}, bf16[5120]{0:T(1024)(128)(2,1)}, u32[]{:S(2)}) copy-start(bf16[5120]{0:T(1024)(128)(2,1)} %param.41) | copy-start | bytes 30724
  698.3 35.3 %copy-start.15 = (bf16[5120]{0:T(1024)(128)(2,1)S(1)}, bf16[5120]{0:T(1024)(128)(2,1)}, u32[]{:S(2)}) copy-start(bf16[5120]{0:T(1024)(128)(2,1)} %param.45) | copy-start | bytes 30724
  698.3 35.3 %copy-start.16 = (bf16[5120]{0:T(1024)(128)(2,1)S(1)}, bf16[5120]{0:T(1024)(128)(2,1)}, u32[]{:S(2)}) copy-start(bf16[5120]{0:T(1024)(128)(2,1)} %param.46) | copy-start | bytes 30724
  698.3 35.3 %copy-start.17 = (f32[512]{0:T(512)S(1)}, f32[512]{0:T(512)}, u32[]{:S(2)}) copy-start(f32[512]{0:T(512)} %get-tuple-element.25) | copy-start | bytes 6148
  733.6 28.5 %copy-start.1 = (bf16[1,288,5120]{2,1,0:T(8,128)(2,1)S(1)}, bf16[1,288,5120]{2,1,0:T(8,128)(2,1)}, u32[]{:S(2)}) copy-start(bf16[1,288,5120]{2,1,0:T(8,128)(2,1)} %param.25) | copy-start | bytes 8847364
  733.6 28.5 %copy-start.6 = (f32[1,1,5120]{2,0,1:T(1,128)S(1)}, f32[1,1,5120]{2,0,1:T(1,128)}, u32[]{:S(2)}) copy-start(f32[1,1,5120]{2,0,1:T(1,128)} %get-tuple-element.16) | copy-start | bytes 61444
  885.5 3.5 copy-start.4
  885.5 3.5 copy-start.5
  889.0 59.3 %copy-start.3 = (f32[1,1,5120]{2,0,1:T(1,128)S(1)}, f32[1,1,5120]{2,0,1:T(1,128)}, u32[]{:S(2)}) copy-start(f32[1,1,5120]{2,0,1:T(1,128)} %get-tuple-element.11) | copy-start | bytes 61444
Sparse Core Ops, SparseCore 0:
  209.5 202.8 all-gather.4
  414.0 203.9 all-gather.2
where the time goes:
time: 1030 us; the launch traced here: 1010 us
  matrix products  514 us (50%)
  waiting for transfers between devices  191 us (19%)
  other arithmetic  145 us (14%)
  local copies, waits for them, and re-layouts  98 us (10%)
  blocking collectives  38.4 us (4%)
  starting transfers between devices  14.6 us (1%)
  between operations  14.2 us (1%)
    dot_general x10, matrix products, project(): return jnp.dot(operand, weight, preferred_element_type=jnp.float32)  345 us
    all_gather x1, waiting for transfers between devices, local_block(): k_all = lax.all_gather(k_head, 'sp', axis=1, tiled=True)  97.7 us
    dot_general x2, matrix products, attention(): jnp.einsum('bqhd,bkhd->bhqk', q_b, k_b, preferred_element_type=jnp.float32)  87.3 us
    dot_general x2, matrix products, attention(): jnp.einsum('bhqk,bkhd->bqhd', weights.astype(jnp.bfloat16), v_b, preferre...  81.3 us
    reduce_sum x2, other arithmetic, attention(): weight_sum = jnp.sum(weights, axis=-1)  75.2 us
    all_gather x1, waiting for transfers between devices, local_block(): v_all = lax.all_gather(v_head, 'sp', axis=1, tiled=True)  68.9 us
    all_to_all x1, blocking collectives, local_block(): k_head = lax.all_to_all(k_tok, 'uly', 2, 1, tiled=True)  38.4 us
    another operation x1, other arithmetic  23.4 us
  transfers between devices with their start and end apart: 5, of which 4 were waited for; matrix products, arithmetic and copies ran while one was open for 26% of the time, Pallas kernels for 0%

commit v1 on v0

v1 whole, which is shorter than its diff:
```python
import functools

import jax
import jax.numpy as jnp
from jax import lax
from jax.experimental import pallas as pl
from jax.experimental.pallas import tpu as pltpu
from jax.sharding import PartitionSpec as P

EPS = 1e-6
HEAD = 128
LOG2E = 1.4426950408889634
SM_C = (HEAD ** -0.5) * LOG2E
MESH = pl.DeviceIdType.MESH
CHIPS = 8
VMEM_LIMIT = 64 * 1000 * 1024
F32 = jnp.float32
BF16 = jnp.bfloat16

(R_SH1, R_SC1, R_G1, R_SH2, R_SC2, R_G2, R_BQ, R_BK, R_BV, R_BO, R_GQ, R_GK, R_NW, R_NB, R_CGQ, R_CGK) = range(16)


def dot(a, b):
    return jnp.dot(a, b, preferred_element_type=F32)


def dot_nt(a, b):
    return lax.dot_general(a, b, (((1,), (1,)), ((), ())), preferred_element_type=F32)


def my_place():
    uly = lax.axis_index('uly')
    chip = lax.axis_index('sp') * 2 + uly // 2
    return chip, lax.rem(uly, 2)


def device_at(chip, core):
    return {'sp': chip // 2, 'uly': lax.rem(chip, 2) * 2 + core}


def flip(chip, r):
    out = 0
    for bit in (1, 2, 4):
        out = out + lax.rem(chip // bit + r // bit, 2) * bit
    return out


def meet(me, core, sibling):
    barrier = pltpu.get_barrier_semaphore()
    for r in range(1, CHIPS):
        pl.semaphore_signal(barrier, inc=1, device_id=device_at(flip(me, r), core), device_id_type=MESH)
    if sibling:
        pl.semaphore_signal(barrier, inc=1, device_id=device_at(me, 1 - core), device_id_type=MESH)
    return barrier, CHIPS - 1 + int(sibling)


class Ring:
    def __init__(self, slots, sems, phases):
        self.slots, self.sems, self.phases = slots, sems, phases
        self.depth = slots.shape[0]
        self.base = [sum(p[0] for p in phases[:i]) for i in range(len(phases) + 1)]

    def copies(self, phase, tile, slot):
        n, w_ref, k_rows, n_cols, k_parts, shift = self.phases[phase]
        cols = cols_of(lax.rem(tile // k_parts + shift, n // k_parts), n_cols)
        row0 = lax.rem(tile, k_parts) * k_rows
        quarter = k_rows // 4
        out = []
        for c in range(4):
            rows = pl.ds(pl.multiple_of(row0 + c * quarter, quarter), quarter)
            out.append(pltpu.make_async_copy(w_ref.at[rows, cols], self.slots.at[slot, pl.ds(c * quarter, quarter)], self.sems.at[slot]))
        return out

    def start(self, phase, tile):
        slot = lax.rem(self.base[phase] + tile, self.depth)
        for c in self.copies(phase, tile, slot):
            c.start()

    def prime(self):
        for i in range(self.depth - 1):
            self.start(0, i)

    def take(self, phase, tile):
        n = self.phases[phase][0]
        slot = lax.rem(self.base[phase] + tile, self.depth)
        for c in self.copies(phase, tile, slot):
            c.wait()
        ahead = tile + self.depth - 1

        @pl.when(ahead < n)
        def _():
            self.start(phase, ahead)

        if phase + 1 < len(self.phases):
            @pl.when(ahead >= n)
            def _():
                self.start(phase + 1, ahead - n)
        return slot


def cols_of(i, width):
    return pl.ds(pl.multiple_of(i * width, width), width)


def add_squares(ss_ref, rows, acc):
    total = ss_ref[0:rows, :]
    for j in range(acc.shape[1] // 128):
        part = acc[:, j * 128:(j + 1) * 128]
        total = total + part * part
    ss_ref[0:rows, :] = total


def rms_scale(ss_ref, rows, width):
    mean = jnp.sum(ss_ref[0:rows, :], axis=1, keepdims=True) * (1.0 / width)
    ss_ref[0:rows, :] = jnp.broadcast_to(lax.rsqrt(mean + EPS), (rows, 128))


def layer_norm_rows(x_f32, mul, add):
    width = x_f32.shape[1]
    mean = jnp.sum(x_f32, axis=1, keepdims=True) * (1.0 / width)
    centered = x_f32 - mean
    var = jnp.sum(centered * centered, axis=1, keepdims=True) * (1.0 / width)
    return (centered * lax.rsqrt(var + EPS)) * mul + add


def qkv_kernel(x_ref, par_ref, cos_ref, sin_ref, ctx_ref, wv_ref, wk_ref, wq_ref, cwk_ref, cwv_ref,
               q_out, k_out, v_out, ck_out, cv_out,
               y_ref, h_ref, ss_ref, qkv_ref, stage_ref, ring_ref, ring_sem, out_sem, stage_sem, send_sem, recv_sem):
    rows, width = x_ref.shape
    text = ctx_ref.shape[0]
    tn = ring_ref.shape[2]
    nt = width // tn
    part = width // CHIPS
    me, core = my_place()
    barrier, n_signals = meet(me, core, False)
    shift = (nt // 2) * (1 - me // (CHIPS // 2))
    ring = Ring(ring_ref, ring_sem, [(nt, w, width, tn, 1, sh) for w, sh in ((wv_ref, shift), (wk_ref, 0), (wq_ref, 0), (cwk_ref, 0), (cwv_ref, 0))])
    ring.prime()

    def norm_block(i, _):
        r = pl.ds(pl.multiple_of(i * 16, 16), 16)
        x = x_ref[r, :].astype(F32)
        y_ref[r, :] = layer_norm_rows(x, 1.0 + par_ref[R_SC1:R_SC1 + 1, :], par_ref[R_SH1:R_SH1 + 1, :]).astype(BF16)
        return 0

    lax.fori_loop(0, rows // 16, norm_block, 0)
    pl.semaphore_wait(barrier, n_signals)

    def remote(n, dst, r):
        to = flip(me, r)
        return pltpu.make_async_remote_copy(
            src_ref=qkv_ref.at[n, :, cols_of(to, part)], dst_ref=dst.at[cols_of(me, rows)],
            send_sem=send_sem.at[n, r], recv_sem=recv_sem.at[n, r], device_id=device_at(to, core), device_id_type=MESH)

    def local(n, dst):
        return pltpu.make_async_copy(qkv_ref.at[n, :, cols_of(me, part)], dst.at[cols_of(me, rows)], out_sem.at[n])

    def q_copies():
        return [pltpu.make_async_copy(qkv_ref.at[2, :, pl.ds(d * part, part)], q_out.at[d], out_sem.at[2]) for d in range(CHIPS)]

    def v_tile(i, _):
        slot = ring.take(0, i)

        @pl.when(i == nt // 2)
        def _():
            for r in range(CHIPS // 2, CHIPS):
                remote(0, v_out, r).start()

        cols = cols_of(lax.rem(i + shift, nt), tn)
        qkv_ref[0, :, cols] = (dot(y_ref[...], ring_ref[slot]) + par_ref[R_BV:R_BV + 1, cols]).astype(BF16)
        return 0

    lax.fori_loop(0, nt, v_tile, 0)

    def v_rest():
        for r in range(1, CHIPS // 2):
            remote(0, v_out, r).start()
        local(0, v_out).start()

    def k_all():
        for r in range(1, CHIPS):
            remote(1, k_out, r).start()
        local(1, k_out).start()

    def q_all():
        for c in q_copies():
            c.start()

    def normed_phase(phase, n, row_b, row_g, send_last):
        ss_ref[0:rows, :] = jnp.zeros((rows, 128), F32)

        def tile(i, _):
            slot = ring.take(phase, i)
            pl.when(i == 0)(send_last)
            cols = cols_of(i, tn)
            acc = dot(y_ref[...], ring_ref[slot]) + par_ref[row_b:row_b + 1, cols]
            h_ref[0:rows, cols] = acc
            add_squares(ss_ref, rows, acc)
            return 0

        lax.fori_loop(0, nt, tile, 0)
        rms_scale(ss_ref, rows, width)
        even = lax.rem(lax.broadcasted_iota(jnp.int32, (rows, HEAD), 1), 2) == 0

        def head(j, _):
            cols = cols_of(j, HEAD)
            x = (h_ref[0:rows, cols] * ss_ref[0:rows, :]) * par_ref[row_g:row_g + 1, cols]
            other = jnp.where(even, pltpu.roll(x, HEAD - 1, 1), pltpu.roll(x, 1, 1))
            qkv_ref[n, :, cols] = (x * cos_ref[...] + other * sin_ref[...]).astype(BF16)
            return 0

        lax.fori_loop(0, width // HEAD, head, 0)

    normed_phase(1, 1, R_BK, R_GK, v_rest)
    normed_phase(2, 2, R_BQ, R_GQ, k_all)

    def stage_copy(i, slot, dst):
        return pltpu.make_async_copy(stage_ref.at[slot], dst.at[:, cols_of(i, tn)], stage_sem.at[slot])

    ss_ref[...] = jnp.zeros_like(ss_ref)

    def ck_tile(i, _):
        slot = ring.take(3, i)
        pl.when(i == 0)(q_all)
        acc = dot(ctx_ref[...], ring_ref[slot])
        h_ref[:, cols_of(i, tn)] = acc
        add_squares(ss_ref, text, acc)
        return 0

    lax.fori_loop(0, nt, ck_tile, 0)
    rms_scale(ss_ref, text, width)

    def ck_norm(i, _):
        s = lax.rem(i, 2)

        @pl.when(i >= 2)
        def _():
            stage_copy(i, s, ck_out).wait()

        for j in range(tn // HEAD):
            cols = pl.ds(pl.multiple_of(i * tn + j * HEAD, HEAD), HEAD)
            stage_ref[s, :, j * HEAD:(j + 1) * HEAD] = ((h_ref[:, cols] * ss_ref[...]) * par_ref[R_CGK:R_CGK + 1, cols]).astype(BF16)
        stage_copy(i, s, ck_out).start()
        return 0

    lax.fori_loop(0, nt, ck_norm, 0)

    def cv_tile(i, _):
        slot = ring.take(4, i)
        s = lax.rem(nt + i, 2)
        stage_copy(i, s, cv_out).wait()
        stage_ref[s] = dot(ctx_ref[...], ring_ref[slot]).astype(BF16)
        stage_copy(i, s, cv_out).start()
        return 0

    lax.fori_loop(0, nt, cv_tile, 0)
    for i in range(2):
        stage_copy(0, i, cv_out).wait()
    for c in q_copies():
        c.wait()
    for n, dst in ((0, v_out), (1, k_out)):
        local(n, dst).wait()
        for r in range(1, CHIPS):
            remote(n, dst, r).wait()


def any_spec():
    return pl.BlockSpec(memory_space=pl.ANY)


def vmem_spec():
    return pl.BlockSpec(memory_space=pltpu.VMEM)


def qkv_call(x, par, cos, sin, ctx, wv, wk, wq, cwk, cwv, tn):
    rows, width = x.shape
    text = ctx.shape[0]
    part = width // CHIPS
    split = jax.ShapeDtypeStruct((CHIPS, rows, part), BF16)
    gathered = jax.ShapeDtypeStruct((CHIPS * rows, part), BF16)
    flops = 2 * width * width * (3 * rows + 2 * text)
    return pl.pallas_call(
        qkv_kernel,
        out_shape=(split, gathered, gathered, jax.ShapeDtypeStruct((text, width), BF16), jax.ShapeDtypeStruct((text, width), BF16)),
        in_specs=[vmem_spec()] * 5 + [any_spec()] * 5,
        out_specs=[any_spec()] * 5,
        scratch_shapes=[
            pltpu.VMEM((rows, width), BF16),
            pltpu.VMEM((text, width), F32),
            pltpu.VMEM((text, 128), F32),
            pltpu.VMEM((3, rows, width), BF16),
            pltpu.VMEM((2, text, tn), BF16),
            pltpu.VMEM((3, width, tn), BF16),
            pltpu.SemaphoreType.DMA((3,)),
            pltpu.SemaphoreType.DMA((3,)),
            pltpu.SemaphoreType.DMA((2,)),
            pltpu.SemaphoreType.DMA((2, CHIPS)),
            pltpu.SemaphoreType.DMA((2, CHIPS)),
        ],
        compiler_params=pltpu.CompilerParams(vmem_limit_bytes=VMEM_LIMIT, collective_id=0, has_side_effects=True),
        cost_estimate=pl.CostEstimate(flops=flops, bytes_accessed=10 * width * width, transcendentals=0),
        name='qkv',
    )(x, par, cos, sin, ctx, wv, wk, wq, cwk, cwv)


def attend_kernel(q_ref, k_ref, v_ref, o_out, kbuf, vbuf, qbuf, obuf, s0_ref, s1_ref, mx0_ref, mx1_ref,
                  own_sem, pair_send, pair_recv, q_send, q_recv, o_send, o_recv):
    n_heads, keys, _ = kbuf.shape
    half = keys // 2
    rows = qbuf.shape[1]
    blocks = CHIPS * n_heads
    kb = 512 if keys % 512 == 0 else keys
    n_kb = keys // kb
    me, core = my_place()
    barrier, n_signals = meet(me, core, True)

    def own(h):
        return [pltpu.make_async_copy(src.at[:, cols_of(h, HEAD)], dst.at[h, 0:half, :], own_sem.at[n, h])
                for n, (src, dst) in enumerate(((k_ref, kbuf), (v_ref, vbuf)))]

    def pair(h):
        return [pltpu.make_async_remote_copy(
            src_ref=src.at[:, cols_of(h, HEAD)], dst_ref=dst.at[h, pl.ds(half, half), :],
            send_sem=pair_send.at[n, h], recv_sem=pair_recv.at[n, h], device_id=device_at(me, 1 - core), device_id_type=MESH)
            for n, (src, dst) in enumerate(((k_ref, kbuf), (v_ref, vbuf)))]

    def q_local():
        return pltpu.make_async_copy(q_ref.at[me], qbuf.at[0], q_recv.at[0])

    def q_remote(r):
        to = flip(me, r)
        return pltpu.make_async_remote_copy(
            src_ref=q_ref.at[to], dst_ref=qbuf.at[r], send_sem=q_send.at[r], recv_sem=q_recv.at[r],
            device_id=device_at(to, core), device_id_type=MESH)

    def o_local(h):
        cols = cols_of(h, HEAD)
        return pltpu.make_async_copy(obuf.at[0, :, cols], o_out.at[me, :, cols], o_send.at[0, h])

    def o_remote(r, h):
        cols = cols_of(h, HEAD)
        return pltpu.make_async_remote_copy(
            src_ref=obuf.at[r, :, cols], dst_ref=o_out.at[me, :, cols], send_sem=o_send.at[r, h], recv_sem=o_recv.at[r, h],
            device_id=device_at(flip(me, r), core), device_id_type=MESH)

    q_local().start()
    for h in range(n_heads):
        for c in own(h):
            c.start()
    pl.semaphore_wait(barrier, n_signals)
    for c in pair(0):
        c.start()
    for r in range(1, CHIPS):
        q_remote(r).start()
    for h in range(1, n_heads):
        for c in pair(h):
            c.start()

    def send_output(b):
        r, h = b // n_heads, lax.rem(b, n_heads)

        @pl.when(r == 0)
        def _():
            o_local(h).start()

        @pl.when(r > 0)
        def _():
            o_remote(r, h).start()

    def step(i, now, before):
        s_now, mx_now = now
        cur = jnp.minimum(i, blocks - 1)
        r, h = cur // n_heads, lax.rem(cur, n_heads)

        @pl.when(i < n_heads)
        def _():
            for c in own(h):
                c.wait()
            for c in pair(h):
                c.wait_recv()

        @pl.when(i == 0)
        def _():
            q_local().wait()

        @pl.when((i > 0) & (i < blocks) & (h == 0))
        def _():
            q_remote(r).wait_recv()

        if before is not None:
            @pl.when(i >= 2)
            def _():
                send_output(i - 2)

            s_old, mx_old = before
            old_r, old_h = (i - 1) // n_heads, lax.rem(i - 1, n_heads)
            total = jnp.zeros((rows, 128), F32)
            acc = jnp.zeros((rows, HEAD), F32)
        q = qbuf[r, :, cols_of(h, HEAD)]
        mx = None
        for j in range(n_kb):
            s = dot_nt(q, kbuf[h, j * kb:(j + 1) * kb, :])
            s_now[:, j * kb:(j + 1) * kb] = s
            for g in range(kb // 128):
                sg = s[:, g * 128:(g + 1) * 128]
                mx = sg if mx is None else jnp.maximum(mx, sg)
            if before is not None:
                parts = []
                for g in range(kb // 128):
                    c0 = j * kb + g * 128
                    p = jnp.exp2((s_old[:, c0:c0 + 128] - mx_old[...]) * SM_C)
                    total = total + p
                    parts.append(p.astype(BF16))
                acc = acc + dot(jnp.concatenate(parts, axis=1), vbuf[old_h, j * kb:(j + 1) * kb, :])
        mx_now[...] = jnp.broadcast_to(jnp.max(mx, axis=1, keepdims=True), (rows, 128))
        if before is not None:
            obuf[old_r, :, cols_of(old_h, HEAD)] = (acc / jnp.sum(total, axis=1, keepdims=True)).astype(BF16)

    bufs = ((s0_ref, mx0_ref), (s1_ref, mx1_ref))
    step(jnp.int32(0), bufs[0], None)

    def pair_of_steps(t, _):
        step(2 * t + 1, bufs[1], bufs[0])
        step(2 * t + 2, bufs[0], bufs[1])
        return 0

    lax.fori_loop(0, blocks // 2, pair_of_steps, 0)
    send_output(jnp.int32(blocks - 1))

    for h in range(n_heads):
        for c in pair(h):
            c.wait_send()
        o_local(h).wait()

    def drain(r, _):
        q_remote(r).wait_send()
        for h in range(n_heads):
            o_remote(r, h).wait()
        return 0

    lax.fori_loop(1, CHIPS, drain, 0)


def attend_call(q, k, v):
    _, rows, part = q.shape
    half = k.shape[0]
    n_heads = part // HEAD
    flops = 8 * half * half * part
    return pl.pallas_call(
        attend_kernel,
        out_shape=jax.ShapeDtypeStruct((CHIPS, rows, part), BF16),
        in_specs=[any_spec()] * 3,
        out_specs=any_spec(),
        scratch_shapes=[
            pltpu.VMEM((n_heads, 2 * half, HEAD), BF16),
            pltpu.VMEM((n_heads, 2 * half, HEAD), BF16),
            pltpu.VMEM((CHIPS, rows, part), BF16),
            pltpu.VMEM((CHIPS, rows, part), BF16),
            pltpu.VMEM((rows, 2 * half), F32),
            pltpu.VMEM((rows, 2 * half), F32),
            pltpu.VMEM((rows, 128), F32),
            pltpu.VMEM((rows, 128), F32),
            pltpu.SemaphoreType.DMA((2, n_heads)),
            pltpu.SemaphoreType.DMA((2, n_heads)),
            pltpu.SemaphoreType.DMA((2, n_heads)),
            pltpu.SemaphoreType.DMA((CHIPS,)),
            pltpu.SemaphoreType.DMA((CHIPS,)),
            pltpu.SemaphoreType.DMA((CHIPS, n_heads)),
            pltpu.SemaphoreType.DMA((CHIPS, n_heads)),
        ],
        compiler_params=pltpu.CompilerParams(vmem_limit_bytes=VMEM_LIMIT, collective_id=1, has_side_effects=True),
        cost_estimate=pl.CostEstimate(flops=flops, bytes_accessed=8 * half * part, transcendentals=2 * half * half * n_heads),
        name='attend',
    )(q, k, v)


def tail_kernel(x_ref, par_ref, o_ref, ck_ref, cv_ref, wo_ref, cwq_ref, cwo_ref, w1_ref, w2_ref, out_ref,
                a_ref, b_ref, xf_ref, h_ref, u_ref, ss_ref, kbuf, vbuf, stage_ref, ring_ref,
                ring_sem, in_sem, kv_sem, stage_sem):
    rows, width = x_ref.shape
    ff = u_ref.shape[1]
    tn = ring_ref.shape[2]
    nt = width // tn
    n_ff = ff // tn
    k_parts = 1
    while ff // k_parts > width or ff % k_parts:
        k_parts += 1
    kc = ff // k_parts
    part = width // CHIPS
    ring = Ring(ring_ref, ring_sem, [
        (nt, wo_ref, width, tn, 1, 0), (nt, cwq_ref, width, tn, 1, 0), (nt, cwo_ref, width, tn, 1, 0),
        (n_ff, w1_ref, width, tn, 1, 0), (nt * k_parts, w2_ref, kc, tn, k_parts, 0)])
    o_copies = [pltpu.make_async_copy(o_ref.at[d], a_ref.at[:, pl.ds(d * part, part)], in_sem) for d in range(CHIPS)]
    for c in o_copies:
        c.start()
    ring.prime()
    for c in o_copies:
        c.wait()

    def o_tile(i, _):
        slot = ring.take(0, i)
        cols = cols_of(i, tn)
        acc = dot(a_ref[...], ring_ref[slot]) + par_ref[R_BO:R_BO + 1, cols]
        xf_ref[:, cols] = x_ref[:, cols].astype(F32) + par_ref[R_G1:R_G1 + 1, cols] * acc
        return 0

    lax.fori_loop(0, nt, o_tile, 0)

    def norm_to(dst, mul, add):
        def block(i, _):
            r = pl.ds(pl.multiple_of(i * 16, 16), 16)
            dst[r, :] = layer_norm_rows(xf_ref[r, :], mul(), add()).astype(BF16)
            return 0

        lax.fori_loop(0, rows // 16, block, 0)

    norm_to(b_ref, lambda: par_ref[R_NW:R_NW + 1, :], lambda: par_ref[R_NB:R_NB + 1, :])
    ss_ref[...] = jnp.zeros_like(ss_ref)

    def cq_tile(i, _):
        slot = ring.take(1, i)
        acc = dot(b_ref[...], ring_ref[slot])
        h_ref[:, cols_of(i, tn)] = acc
        add_squares(ss_ref, rows, acc)
        return 0

    lax.fori_loop(0, nt, cq_tile, 0)
    rms_scale(ss_ref, rows, width)

    def cq_head(j, _):
        cols = cols_of(j, HEAD)
        a_ref[:, cols] = ((h_ref[:, cols] * ss_ref[...]) * par_ref[R_CGQ:R_CGQ + 1, cols]).astype(BF16)
        return 0

    gw = kbuf.shape[2]
    n_groups = width // gw
    heads = gw // HEAD

    def kv_loads(g, slot):
        cols = cols_of(g, gw)
        return (pltpu.make_async_copy(ck_ref.at[:, cols], kbuf.at[slot], kv_sem.at[0, slot]),
                pltpu.make_async_copy(cv_ref.at[:, cols], vbuf.at[slot], kv_sem.at[1, slot]))

    for c in kv_loads(0, 0):
        c.start()
    lax.fori_loop(0, width // HEAD, cq_head, 0)

    def cross_group(g, _):
        slot = lax.rem(g, 2)
        for c in kv_loads(g, slot):
            c.wait()

        @pl.when(g + 1 < n_groups)
        def _():
            for c in kv_loads(g + 1, 1 - slot):
                c.start()

        for j in range(heads):
            cols = pl.ds(pl.multiple_of(g * gw + j * HEAD, HEAD), HEAD)
            hs = slice(j * HEAD, (j + 1) * HEAD)
            s = dot_nt(a_ref[:, cols], kbuf[slot, :, hs])
            m = jnp.max(s, axis=1, keepdims=True)
            p = jnp.exp2((s - m) * SM_C)
            total = jnp.sum(p, axis=1, keepdims=True)
            b_ref[:, cols] = (dot(p.astype(BF16), vbuf[slot, :, hs]) / total).astype(BF16)
        return 0

    lax.fori_loop(0, n_groups, cross_group, 0)

    def co_tile(i, _):
        slot = ring.take(2, i)
        cols = cols_of(i, tn)
        xf_ref[:, cols] = xf_ref[:, cols] + dot(b_ref[...], ring_ref[slot])
        return 0

    lax.fori_loop(0, nt, co_tile, 0)
    norm_to(a_ref, lambda: 1.0 + par_ref[R_SC2:R_SC2 + 1, :], lambda: par_ref[R_SH2:R_SH2 + 1, :])

    def f1_tile(i, _):
        slot = ring.take(3, i)
        acc = dot(a_ref[...], ring_ref[slot])
        u_ref[:, cols_of(i, tn)] = jax.nn.gelu(acc, approximate=True).astype(BF16)
        return 0

    lax.fori_loop(0, n_ff, f1_tile, 0)

    def stage_copy(i, slot):
        return pltpu.make_async_copy(stage_ref.at[slot], out_ref.at[:, cols_of(i, tn)], stage_sem.at[slot])

    def f2_tile(i, _):
        s = lax.rem(i, 2)

        @pl.when(i >= 2)
        def _():
            stage_copy(i, s).wait()

        acc = None
        for c in range(k_parts):
            slot = ring.take(4, i * k_parts + c)
            term = dot(u_ref[:, c * kc:(c + 1) * kc], ring_ref[slot, 0:kc, :])
            acc = term if acc is None else acc + term
        cols = cols_of(i, tn)
        stage_ref[s] = (xf_ref[:, cols] + par_ref[R_G2:R_G2 + 1, cols] * acc).astype(BF16)
        stage_copy(i, s).start()
        return 0

    lax.fori_loop(0, nt, f2_tile, 0)
    for i in range(2):
        stage_copy(0, i).wait()


def tail_call(x, par, o, ck, cv, wo, cwq, cwo, w1, w2, tn):
    rows, width = x.shape
    text = ck.shape[0]
    ff = w1.shape[1]
    flops = 2 * rows * width * (3 * width + 2 * ff) + 4 * rows * text * width
    return pl.pallas_call(
        tail_kernel,
        out_shape=jax.ShapeDtypeStruct((rows, width), BF16),
        in_specs=[vmem_spec()] * 2 + [any_spec()] * 8,
        out_specs=any_spec(),
        scratch_shapes=[
            pltpu.VMEM((rows, width), BF16),
            pltpu.VMEM((rows, width), BF16),
            pltpu.VMEM((rows, width), F32),
            pltpu.VMEM((rows, width), F32),
            pltpu.VMEM((rows, ff), BF16),
            pltpu.VMEM((rows, 128), F32),
            pltpu.VMEM((2, text, 4 * HEAD), BF16),
            pltpu.VMEM((2, text, 4 * HEAD), BF16),
            pltpu.VMEM((2, rows, tn), BF16),
            pltpu.VMEM((3, width, tn), BF16),
            pltpu.SemaphoreType.DMA((3,)),
            pltpu.SemaphoreType.DMA,
            pltpu.SemaphoreType.DMA((2, 2)),
            pltpu.SemaphoreType.DMA((2,)),
        ],
        compiler_params=pltpu.CompilerParams(vmem_limit_bytes=VMEM_LIMIT),
        cost_estimate=pl.CostEstimate(flops=flops, bytes_accessed=2 * width * (3 * width + 2 * ff), transcendentals=rows * ff),
        name='tail',
    )(x, par, o, ck, cv, wo, cwq, cwo, w1, w2)


def solution(mesh):
    tok_spec = P('dp', ('sp', 'uly'), None)
    batch_spec = P('dp', None, None)

    def local_block(tokens, rope_ang, t_emb, block_mod, context, attn_wq, attn_bq, attn_wk, attn_bk, attn_wv, attn_bv, attn_gq, attn_gk, attn_wo, attn_bo, norm3_w, norm3_b, cross_wq, cross_wk, cross_wv, cross_gq, cross_gk, cross_wo, ffn_w1, ffn_w2):
        x = tokens[0]
        tn = 512
        vectors = jnp.stack([attn_bq, attn_bk, attn_bv, attn_bo, attn_gq, attn_gk, norm3_w, norm3_b, cross_gq, cross_gk]).astype(F32)
        par = jnp.concatenate([t_emb[0] + block_mod[0], vectors], axis=0)
        lane = jnp.arange(HEAD)
        spread = (lane[None, :] // 2 == jnp.arange(HEAD // 2)[:, None]).astype(F32)
        sign = jnp.where(lane % 2 == 0, -1.0, 1.0).astype(F32)
        cos = jnp.dot(jnp.cos(rope_ang), spread, precision=lax.Precision.HIGHEST)
        sin = jnp.dot(jnp.sin(rope_ang), spread * sign[None, :], precision=lax.Precision.HIGHEST)
        q, k, v, ck, cv = qkv_call(x, par, cos, sin, context[0], attn_wv, attn_wk, attn_wq, cross_wk, cross_wv, tn)
        o_own = attend_call(q, k, v)
        out = tail_call(x, par, o_own, ck, cv, attn_wo, cross_wq, cross_wo, ffn_w1, ffn_w2, tn)
        return out[None]

    in_specs = (tok_spec, P(('sp', 'uly'), None), batch_spec, P(), batch_spec) + (P(),) * 20
    return jax.shard_map(local_block, mesh=mesh, in_specs=in_specs, out_specs=tok_spec, check_vma=False)
```

time: 1030 us -> 488 us (0.47); the launches traced: 1010 us -> 486 us
  matrix products: 514 us -> 4.41 us
  Pallas kernels: 0 us -> 472 us
  waiting for transfers between devices: 191 us -> 0 us
  other arithmetic: 145 us -> 1.84 us
  local copies, waits for them, and re-layouts: 98 us -> 7.48 us
  blocking collectives: 38.4 us -> 0 us
  starting transfers between devices: 14.6 us -> 0 us
  between operations: 14.2 us -> 0.22 us
    dot_general x14 -> x2, matrix products: 514 us -> 4.41 us  [the longest x1 2.25 us: local_block(): jnp.dot(jnp.sin(rope_ang), spread * sign[None, :], precision=lax.Precisio...]
    pallas_call x0 -> x3, Pallas kernels: none -> 472 us  [the longest x1 185 us: tail_call(): pl.pallas_call(tail_kernel, out_shape=jax.ShapeDtypeStruct((rows, width),...]
    all_gather x2 -> x0, waiting for transfers between devices: 167 us -> none  [the longest x1 97.7 us: local_block(): k_all = lax.all_gather(k_head, 'sp', axis=1, tiled=True)]
    reduce_sum x6 -> x0, other arithmetic: 87.2 us -> none  [the longest x2 75.2 us: attention(): weight_sum = jnp.sum(weights, axis=-1)]
    another operation x2 -> x0, other arithmetic: 43.2 us -> none
    all_to_all x1 -> x0, blocking collectives: 38.4 us -> none  [local_block(): k_head = lax.all_to_all(k_tok, 'uly', 2, 1, tiled=True)]
    another operation x4 -> x11, local copies, waits for them, and re-layouts: 34.5 us -> 7.48 us  [local_block(): jnp.stack([attn_bq, attn_bk, attn_bv, attn_bo, attn_gq, attn_gk, norm3_w,...]
    all_to_all x3 -> x0, waiting for transfers between devices: 24 us -> none  [the longest x1 18.1 us: local_block(): o_tok = lax.all_to_all(o_head, 'uly', 1, 2, tiled=True)]
  transfers between devices with their start and end apart: 5 -> 0, of which waited for: 4 -> 0; matrix products, arithmetic and copies ran while one was open for 26% -> 0% of each run, Pallas kernels for 0% -> 0%
where the time goes in v1:
time: 488 us; the launch traced here: 486 us
  Pallas kernels  472 us (97%)
  local copies, waits for them, and re-layouts  7.48 us (2%)
    pallas_call x1, Pallas kernels, tail_call(): pl.pallas_call(tail_kernel, out_shape=jax.ShapeDtypeStruct((rows, width),...  185 us
    pallas_call x1, Pallas kernels, qkv_call(): pl.pallas_call(qkv_kernel, out_shape=(split, gathered, gathered, jax.Shap...  154 us
    pallas_call x1, Pallas kernels, attend_call(): pl.pallas_call(attend_kernel, out_shape=jax.ShapeDtypeStruct((CHIPS, rows...  133 us

profile of v1, /device:TPU:8, one launch (start us, length us, event | category | flops | bytes accessed | tf_op | source)
XLA Modules:
  0.0 485.8 jit_solution(914849685950981870)
XLA Ops:
  0.0 0.7 stack.33
  0.7 0.7 stack.34
  1.5 0.7 stack.35
  2.2 0.7 stack.37
  2.9 0.7 stack.38
  3.6 0.7 stack.36
  4.3 0.7 stack.39
  5.1 0.7 stack.40
  5.8 0.7 stack.41
  6.5 0.7 stack.42
  7.2 0.3 stack.43
  7.5 2.2 convolution_bitcast_fusion.sin_ref
  9.8 2.2 convolution_bitcast_fusion.1.cos_ref
  12.0 1.0 fusion
  13.0 0.8 pad_maximum_fusion.par_ref
  13.8 154.0 %qkv.1 = (bf16[8,288,640]{2,1,0:T(8,128)(2,1)}, bf16[2304,640]{1,0:T(8,128)(2,1)}, bf16[2304,640]{1,0:T(8,128)(2,1)}, bf16[512,5120]{1,0:T(8,128)(2,1)}, bf16[512,5120]{1,0:T(8,128)(2,1)}) custom-call(bf16[288,5120]{1,0:T(8,128)(2,1)} %bitcast.10, f32[16,5120]{1,0:T(8,128)} %pad_maximum_fusion.par_ref, f32[288,128]{1,0:T(8,128)} %convolution_bitcast_fusion.1.cos_ref, ...), custom_call_target="tpu_custom_call" | custom-call | flops 98985574400 | bytes 262144000 | tf_op jit(solution)/shard_map/qkv/pallas_call | solution.py:282
  167.8 133.2 %attend.1.o_ref = bf16[8,288,640]{2,1,0:T(8,128)(2,1)} custom-call(bf16[8,288,640]{2,1,0:T(8,128)(2,1)} %get-tuple-element.10.q_ref, bf16[2304,640]{1,0:T(8,128)(2,1)} %get-tuple-element.11.k_ref, bf16[2304,640]{1,0:T(8,128)(2,1)} %get-tuple-element.12.v_ref), custom_call_target="tpu_custom_call" | custom-call | flops 27179089920 | bytes 11796480 | tf_op jit(solution)/shard_map/attend/pallas_call | solution.py:449
  301.0 184.7 %tail.1 = bf16[288,5120]{1,0:T(8,128)(2,1)} custom-call(bf16[288,5120]{1,0:T(8,128)(2,1)} %bitcast.11, f32[16,5120]{1,0:T(8,128)} %pad_maximum_fusion.par_ref, bf16[8,288,640]{2,1,0:T(8,128)(2,1)} %attend.1.o_ref, bf16[512,5120]{1,0:T(8,128)(2,1)} %get-tuple-element.13.ck_ref, bf16[512,5120]{1,0:T(8,128)(2,1)} %get-tuple-element.14.cv_ref, ...), custom_call_target="tpu_custom_call" | custom-call | flops 129855651840 | bytes 440401920 | tf_op jit(solution)/shard_map/tail/pallas_call | solution.py:617
  (3 shorter events, 0.0 us)

commit v2 on v1

v2 whole, which is shorter than its diff:
```python
import functools

import jax
import jax.numpy as jnp
from jax import lax
from jax.experimental import pallas as pl
from jax.experimental.pallas import tpu as pltpu
from jax.sharding import PartitionSpec as P

EPS = 1e-6
HEAD = 128
LOG2E = 1.4426950408889634
SM_C = (HEAD ** -0.5) * LOG2E
MESH = pl.DeviceIdType.MESH
CHIPS = 8
VMEM_LIMIT = 64 * 1000 * 1024
F32 = jnp.float32
BF16 = jnp.bfloat16

SH1, SC1, G1, SH2, SC2, G2 = range(6)


def dot(a, b):
    return jnp.dot(a, b, preferred_element_type=F32)


def dot_nt(a, b):
    return lax.dot_general(a, b, (((1,), (1,)), ((), ())), preferred_element_type=F32)


def my_place():
    uly = lax.axis_index('uly')
    chip = lax.axis_index('sp') * 2 + uly // 2
    return chip, lax.rem(uly, 2)


def device_at(chip, core):
    return {'sp': chip // 2, 'uly': lax.rem(chip, 2) * 2 + core}


def flip(chip, r):
    out = 0
    for bit in (1, 2, 4):
        out = out + lax.rem(chip // bit + r // bit, 2) * bit
    return out


def meet(me, core, sibling):
    barrier = pltpu.get_barrier_semaphore()
    for r in range(1, CHIPS):
        pl.semaphore_signal(barrier, inc=1, device_id=device_at(flip(me, r), core), device_id_type=MESH)
    if sibling:
        pl.semaphore_signal(barrier, inc=1, device_id=device_at(me, 1 - core), device_id_type=MESH)
    return barrier, CHIPS - 1 + int(sibling)


class Ring:
    def __init__(self, slots, sems, phases):
        self.slots, self.sems, self.phases = slots, sems, phases
        self.depth = slots.shape[0]
        self.base = [sum(p[0] for p in phases[:i]) for i in range(len(phases) + 1)]

    def slot(self, phase, tile):
        return lax.rem(self.base[phase] + tile, self.depth)

    def copies(self, phase, tile):
        n, w_ref, k_rows, n_cols, k_parts, shift = self.phases[phase]
        slot = self.slot(phase, tile)
        cols = cols_of(lax.rem(tile // k_parts + shift, n // k_parts), n_cols)
        row0 = lax.rem(tile, k_parts) * k_rows
        quarter = k_rows // 4
        out = []
        for c in range(4):
            rows = pl.ds(pl.multiple_of(row0 + c * quarter, quarter), quarter)
            out.append(pltpu.make_async_copy(w_ref.at[rows, cols], self.slots.at[slot, pl.ds(c * quarter, quarter)], self.sems.at[slot]))
        return out

    def start(self, phase, tile):
        for c in self.copies(phase, tile):
            c.start()

    def prime(self):
        for i in range(self.depth):
            if i < self.phases[0][0]:
                self.start(0, i)
            else:
                self.start(1, i - self.phases[0][0])

    def wait(self, phase, tile):
        for c in self.copies(phase, tile):
            c.wait()
        return self.slot(phase, tile)

    def refill(self, phase, tile):
        n = self.phases[phase][0]
        ahead = tile + self.depth

        @pl.when(ahead < n)
        def _():
            self.start(phase, ahead)

        if phase + 1 < len(self.phases):
            @pl.when(ahead >= n)
            def _():
                self.start(phase + 1, ahead - n)


def cols_of(i, width):
    return pl.ds(pl.multiple_of(i * width, width), width)


def groups(acc):
    return [acc[:, g * 128:(g + 1) * 128] for g in range(acc.shape[1] // 128)]


def add_lanes(ref, rows, acc, squares):
    total = ref[0:rows, :]
    for part in groups(acc):
        total = total + (part * part if squares else part)
    ref[0:rows, :] = total


def lane_mean(ref, rows, width):
    return jnp.broadcast_to(jnp.sum(ref[0:rows, :], axis=1, keepdims=True) * (1.0 / width), (rows, 128))


def rms_scale(ss_ref, rows, width):
    ss_ref[0:rows, :] = lax.rsqrt(lane_mean(ss_ref, rows, width) + EPS)


def load_vectors(vec_ref, refs):
    for n, ref in enumerate(refs):
        vec_ref[n] = ref[...].astype(F32)


def layer_norm(load, store, mul, add, rows, width, sum_ref, mean_ref, have_sum):
    step = 4 if width % 512 == 0 else 1
    n = width // 128 // step

    def sums(j, _):
        total = sum_ref[0:rows, :]
        for g in range(step):
            total = total + load(j * step + g)
        sum_ref[0:rows, :] = total
        return 0

    if not have_sum:
        sum_ref[0:rows, :] = jnp.zeros((rows, 128), F32)
        lax.fori_loop(0, n, sums, 0)
    mean_ref[...] = lane_mean(sum_ref, rows, width)
    sum_ref[0:rows, :] = jnp.zeros((rows, 128), F32)

    def squares(j, _):
        total = sum_ref[0:rows, :]
        for g in range(step):
            d = load(j * step + g) - mean_ref[...]
            total = total + d * d
        sum_ref[0:rows, :] = total
        return 0

    lax.fori_loop(0, n, squares, 0)
    rms_scale(sum_ref, rows, width)

    def apply(j, _):
        for g in range(step):
            k = j * step + g
            store(k, ((load(k) - mean_ref[...]) * sum_ref[0:rows, :]) * mul(k) + add(k))
        return 0

    lax.fori_loop(0, n, apply, 0)


def qkv_kernel(x_ref, te_ref, bm_ref, ang_ref, bq_ref, bk_ref, bv_ref, gq_ref, gk_ref, cgk_ref,
               ctx_hbm, wv_ref, wk_ref, wq_ref, cwk_ref,
               q_out, k_out, v_out, ck_out,
               y_ref, h_ref, ss_ref, mean_ref, cos_ref, sin_ref, vec_ref, mod_ref, qkv_ref, ctx_ref, stage_ref, ring_ref,
               ring_sem, out_sem, ctx_sem, stage_sem, send_sem, recv_sem):
    rows, width = x_ref.shape
    text = ctx_ref.shape[0]
    tn = ring_ref.shape[2]
    per = tn // 128
    nt = width // tn
    part = width // CHIPS
    me, core = my_place()
    barrier, n_signals = meet(me, core, False)
    far = (CHIPS // 2) * (1 - me // (CHIPS // 2))
    shift = far * part // tn
    ring = Ring(ring_ref, ring_sem, [(nt, w, width, tn, 1, sh) for w, sh in ((wv_ref, shift), (wk_ref, 0), (wq_ref, 0), (cwk_ref, 0))])
    ring.prime()
    ctx_copy = pltpu.make_async_copy(ctx_hbm, ctx_ref, ctx_sem)
    ctx_copy.start()
    load_vectors(vec_ref, (bq_ref, bk_ref, bv_ref, gq_ref, gk_ref, cgk_ref))
    BQ, BK, BV, GQ, GK, CGK = range(6)
    mod_ref[...] = te_ref[...] + bm_ref[...]

    def vec(n, k):
        return vec_ref[n, pl.ds(k, 1), :]

    def store_y(k, val):
        y_ref[:, cols_of(k, 128)] = val.astype(BF16)

    layer_norm(lambda k: x_ref[:, cols_of(k, 128)].astype(F32), store_y,
               lambda k: 1.0 + mod_ref[SC1:SC1 + 1, cols_of(k, 128)], lambda k: mod_ref[SH1:SH1 + 1, cols_of(k, 128)],
               rows, width, ss_ref, mean_ref, False)
    pl.semaphore_wait(barrier, n_signals)

    def remote(n, dst, r):
        to = flip(me, r)
        return pltpu.make_async_remote_copy(
            src_ref=qkv_ref.at[n, :, cols_of(to, part)], dst_ref=dst.at[cols_of(me, rows)],
            send_sem=send_sem.at[n, r], recv_sem=recv_sem.at[n, r], device_id=device_at(to, core), device_id_type=MESH)

    def local(n, dst):
        return pltpu.make_async_copy(qkv_ref.at[n, :, cols_of(me, part)], dst.at[cols_of(me, rows)], out_sem.at[n])

    def q_copies():
        return [pltpu.make_async_copy(qkv_ref.at[2, :, pl.ds(d * part, part)], q_out.at[d], out_sem.at[2]) for d in range(CHIPS)]

    def v_tile(i, _):
        slot = ring.wait(0, i)
        for j in range(CHIPS // 2):
            @pl.when(i == -(-part * (j + 1) // tn))
            def _():
                remote(0, v_out, flip(me, far + j)).start()

        ct = lax.rem(i + shift, nt)
        for g, a in enumerate(groups(dot(y_ref[...], ring_ref[slot]))):
            k = ct * per + g
            qkv_ref[0, :, cols_of(k, 128)] = (a + vec(BV, k)).astype(BF16)
        ring.refill(0, i)
        return 0

    lax.fori_loop(0, nt, v_tile, 0)

    def v_rest():
        for r in range(1, CHIPS // 2):
            remote(0, v_out, r).start()
        local(0, v_out).start()
        ang = jnp.concatenate([ang_ref[...], ang_ref[...]], axis=1)
        lane = lax.broadcasted_iota(jnp.int32, (rows, HEAD), 1)
        spread = jnp.take_along_axis(ang, lane // 2, axis=1)
        cos_ref[...] = jnp.cos(spread)
        sin_ref[...] = jnp.where(lax.rem(lane, 2) == 0, -1.0, 1.0) * jnp.sin(spread)

    def k_all():
        for r in range(CHIPS - 1, 0, -1):
            remote(1, k_out, r).start()
        local(1, k_out).start()

    def q_all():
        for c in q_copies():
            c.start()
        ctx_copy.wait()

    def normed_phase(phase, n, b, gain, send_last):
        ss_ref[0:rows, :] = jnp.zeros((rows, 128), F32)

        def tile(i, _):
            slot = ring.wait(phase, i)
            pl.when(i == 0)(send_last)
            total = ss_ref[0:rows, :]
            for g, a in enumerate(groups(dot(y_ref[...], ring_ref[slot]))):
                k = i * per + g
                a = a + vec(b, k)
                h_ref[0:rows, cols_of(k, 128)] = a
                total = total + a * a
            ss_ref[0:rows, :] = total
            ring.refill(phase, i)
            return 0

        lax.fori_loop(0, nt, tile, 0)
        rms_scale(ss_ref, rows, width)
        even = lax.rem(lax.broadcasted_iota(jnp.int32, (rows, HEAD), 1), 2) == 0

        def head(j, _):
            cols = cols_of(j, HEAD)
            x = (h_ref[0:rows, cols] * ss_ref[0:rows, :]) * vec(gain, j)
            other = jnp.where(even, pltpu.roll(x, HEAD - 1, 1), pltpu.roll(x, 1, 1))
            qkv_ref[n, :, cols] = (x * cos_ref[...] + other * sin_ref[...]).astype(BF16)
            return 0

        lax.fori_loop(0, width // HEAD, head, 0)

    normed_phase(1, 1, BK, GK, v_rest)
    normed_phase(2, 2, BQ, GQ, k_all)

    def stage_copy(i, slot):
        return pltpu.make_async_copy(stage_ref.at[slot], ck_out.at[:, cols_of(i, tn)], stage_sem.at[slot])

    ss_ref[...] = jnp.zeros_like(ss_ref)

    def ck_tile(i, _):
        slot = ring.wait(3, i)
        pl.when(i == 0)(q_all)
        acc = dot(ctx_ref[...], ring_ref[slot])
        h_ref[:, cols_of(i, tn)] = acc
        add_lanes(ss_ref, text, acc, True)
        ring.refill(3, i)
        return 0

    lax.fori_loop(0, nt, ck_tile, 0)
    rms_scale(ss_ref, text, width)

    def ck_norm(i, _):
        s = lax.rem(i, 2)

        @pl.when(i >= 2)
        def _():
            stage_copy(i, s).wait()

        for j in range(per):
            k = i * per + j
            stage_ref[s, :, j * HEAD:(j + 1) * HEAD] = ((h_ref[:, cols_of(k, 128)] * ss_ref[...]) * vec(CGK, k)).astype(BF16)
        stage_copy(i, s).start()
        return 0

    lax.fori_loop(0, nt, ck_norm, 0)
    for i in range(2):
        stage_copy(0, i).wait()
    for c in q_copies():
        c.wait()
    for n, dst in ((0, v_out), (1, k_out)):
        local(n, dst).wait()
        for r in range(1, CHIPS):
            remote(n, dst, r).wait()


def any_spec():
    return pl.BlockSpec(memory_space=pl.ANY)


def vmem_spec():
    return pl.BlockSpec(memory_space=pltpu.VMEM)


def qkv_call(x, te, bm, ang, vectors, ctx, wv, wk, wq, cwk, tn):
    rows, width = x.shape
    text = ctx.shape[0]
    part = width // CHIPS
    split = jax.ShapeDtypeStruct((CHIPS, rows, part), BF16)
    gathered = jax.ShapeDtypeStruct((CHIPS * rows, part), BF16)
    flops = 2 * width * width * (3 * rows + text)
    return pl.pallas_call(
        qkv_kernel,
        out_shape=(split, gathered, gathered, jax.ShapeDtypeStruct((text, width), BF16)),
        in_specs=[vmem_spec()] * (4 + len(vectors)) + [any_spec()] * 5,
        out_specs=[any_spec()] * 4,
        scratch_shapes=[
            pltpu.VMEM((rows, width), BF16),
            pltpu.VMEM((text, width), F32),
            pltpu.VMEM((text, 128), F32),
            pltpu.VMEM((rows, 128), F32),
            pltpu.VMEM((rows, 128), F32),
            pltpu.VMEM((rows, 128), F32),
            pltpu.VMEM((len(vectors), width // 128, 128), F32),
            pltpu.VMEM(te.shape, F32),
            pltpu.VMEM((3, rows, width), BF16),
            pltpu.VMEM((text, width), BF16),
            pltpu.VMEM((2, text, tn), BF16),
            pltpu.VMEM((3, width, tn), BF16),
            pltpu.SemaphoreType.DMA((3,)),
            pltpu.SemaphoreType.DMA((3,)),
            pltpu.SemaphoreType.DMA,
            pltpu.SemaphoreType.DMA((2,)),
            pltpu.SemaphoreType.DMA((2, CHIPS)),
            pltpu.SemaphoreType.DMA((2, CHIPS)),
        ],
        compiler_params=pltpu.CompilerParams(vmem_limit_bytes=VMEM_LIMIT, collective_id=0, has_side_effects=True),
        cost_estimate=pl.CostEstimate(flops=flops, bytes_accessed=8 * width * width, transcendentals=0),
        name='qkv',
    )(x, te, bm, ang, *vectors, ctx, wv, wk, wq, cwk)


def attend_kernel(q_ref, k_ref, v_ref, ctx_hbm, cwv_ref, o_out, cv_out,
                  kbuf, vbuf, qbuf, obuf, s0_ref, s1_ref, mx0_ref, mx1_ref, ctx_ref, stage_ref, ring_ref,
                  own_sem, pair_send, pair_recv, q_send, q_recv, o_send, o_recv, ctx_sem, stage_sem, ring_sem):
    n_heads, keys, _ = kbuf.shape
    half = keys // 2
    rows = qbuf.shape[1]
    blocks = CHIPS * n_heads
    kb = 512 if keys % 512 == 0 else keys
    n_kb = keys // kb
    me, core = my_place()
    barrier, n_signals = meet(me, core, True)

    def own(h):
        return [pltpu.make_async_copy(src.at[:, cols_of(h, HEAD)], dst.at[h, 0:half, :], own_sem.at[n, h])
                for n, (src, dst) in enumerate(((k_ref, kbuf), (v_ref, vbuf)))]

    def pair(h):
        return [pltpu.make_async_remote_copy(
            src_ref=src.at[:, cols_of(h, HEAD)], dst_ref=dst.at[h, pl.ds(half, half), :],
            send_sem=pair_send.at[n, h], recv_sem=pair_recv.at[n, h], device_id=device_at(me, 1 - core), device_id_type=MESH)
            for n, (src, dst) in enumerate(((k_ref, kbuf), (v_ref, vbuf)))]

    def q_local():
        return pltpu.make_async_copy(q_ref.at[me], qbuf.at[0], q_recv.at[0])

    def q_remote(r):
        to = flip(me, r)
        return pltpu.make_async_remote_copy(
            src_ref=q_ref.at[to], dst_ref=qbuf.at[r], send_sem=q_send.at[r], recv_sem=q_recv.at[r],
            device_id=device_at(to, core), device_id_type=MESH)

    def o_local(h):
        cols = cols_of(h, HEAD)
        return pltpu.make_async_copy(obuf.at[0, :, cols], o_out.at[me, :, cols], o_send.at[0, h])

    def o_remote(r, h):
        cols = cols_of(h, HEAD)
        return pltpu.make_async_remote_copy(
            src_ref=obuf.at[r, :, cols], dst_ref=o_out.at[me, :, cols], send_sem=o_send.at[r, h], recv_sem=o_recv.at[r, h],
            device_id=device_at(flip(me, r), core), device_id_type=MESH)

    q_local().start()
    for h in range(n_heads):
        for c in own(h):
            c.start()
    pl.semaphore_wait(barrier, n_signals)
    for c in pair(0):
        c.start()
    for r in range(1, CHIPS):
        q_remote(r).start()
    for h in range(1, n_heads):
        for c in pair(h):
            c.start()
    tn = ring_ref.shape[2]
    nt = ring_ref.shape[1] // tn
    ring = Ring(ring_ref, ring_sem, [(nt, cwv_ref, ring_ref.shape[1], tn, 1, 0)])
    ring.prime()
    ctx_copy = pltpu.make_async_copy(ctx_hbm, ctx_ref, ctx_sem)
    ctx_copy.start()

    def stage_copy(i, slot):
        return pltpu.make_async_copy(stage_ref.at[slot], cv_out.at[:, cols_of(i, tn)], stage_sem.at[slot])

    def cv_tile(i):
        slot = ring.wait(0, i)
        s = lax.rem(i, 2)

        @pl.when(i == 0)
        def _():
            ctx_copy.wait()

        @pl.when(i >= 2)
        def _():
            stage_copy(i, s).wait()

        stage_ref[s] = dot(ctx_ref[...], ring_ref[slot]).astype(BF16)
        stage_copy(i, s).start()
        ring.refill(0, i)

    def send_output(b):
        r, h = b // n_heads, lax.rem(b, n_heads)

        @pl.when(r == 0)
        def _():
            o_local(h).start()

        @pl.when(r > 0)
        def _():
            o_remote(r, h).start()

    def step(i, now, before):
        s_now, mx_now = now
        cur = jnp.minimum(i, blocks - 1)
        r, h = cur // n_heads, lax.rem(cur, n_heads)

        @pl.when(i < n_heads)
        def _():
            for c in own(h):
                c.wait()
            for c in pair(h):
                c.wait_recv()

        @pl.when(i == 0)
        def _():
            q_local().wait()

        @pl.when((i > 0) & (i < blocks) & (h == 0))
        def _():
            q_remote(r).wait_recv()

        if before is not None:
            @pl.when(i >= 2)
            def _():
                send_output(i - 2)

            s_old, mx_old = before
            old_r, old_h = (i - 1) // n_heads, lax.rem(i - 1, n_heads)
            total = jnp.zeros((rows, 128), F32)
            acc = jnp.zeros((rows, HEAD), F32)
        q = qbuf[r, :, cols_of(h, HEAD)]
        mx = None
        for j in range(n_kb):
            s = dot_nt(q, kbuf[h, j * kb:(j + 1) * kb, :])
            s_now[:, j * kb:(j + 1) * kb] = s
            for g in range(kb // 128):
                sg = s[:, g * 128:(g + 1) * 128]
                mx = sg if mx is None else jnp.maximum(mx, sg)
            if before is not None:
                parts = []
                for g in range(kb // 128):
                    c0 = j * kb + g * 128
                    p = jnp.exp2((s_old[:, c0:c0 + 128] - mx_old[...]) * SM_C)
                    total = total + p
                    parts.append(p.astype(BF16))
                acc = acc + dot(jnp.concatenate(parts, axis=1), vbuf[old_h, j * kb:(j + 1) * kb, :])
        mx_now[...] = jnp.broadcast_to(jnp.max(mx, axis=1, keepdims=True), (rows, 128))
        if before is not None:
            obuf[old_r, :, cols_of(old_h, HEAD)] = (acc / jnp.sum(total, axis=1, keepdims=True)).astype(BF16)

    bufs = ((s0_ref, mx0_ref), (s1_ref, mx1_ref))
    step(jnp.int32(0), bufs[0], None)

    def pair_of_steps(t, _):
        step(2 * t + 1, bufs[1], bufs[0])
        step(2 * t + 2, bufs[0], bufs[1])

        @pl.when((lax.rem(t, every) == 0) & (t < nt * every))
        def _():
            cv_tile(t // every)

        return 0

    every = blocks // 2 // nt
    lax.fori_loop(0, blocks // 2, pair_of_steps, 0)
    send_output(jnp.int32(blocks - 1))
    for i in range(2):
        stage_copy(0, i).wait()

    for h in range(n_heads):
        for c in pair(h):
            c.wait_send()
        o_local(h).wait()

    def drain(r, _):
        q_remote(r).wait_send()
        for h in range(n_heads):
            o_remote(r, h).wait()
        return 0

    lax.fori_loop(1, CHIPS, drain, 0)


def attend_call(q, k, v, ctx, cwv, tn):
    _, rows, part = q.shape
    half = k.shape[0]
    n_heads = part // HEAD
    text, width = ctx.shape
    flops = 8 * half * half * part + 2 * text * width * width
    return pl.pallas_call(
        attend_kernel,
        out_shape=(jax.ShapeDtypeStruct((CHIPS, rows, part), BF16), jax.ShapeDtypeStruct((text, width), BF16)),
        in_specs=[any_spec()] * 5,
        out_specs=[any_spec()] * 2,
        scratch_shapes=[
            pltpu.VMEM((n_heads, 2 * half, HEAD), BF16),
            pltpu.VMEM((n_heads, 2 * half, HEAD), BF16),
            pltpu.VMEM((CHIPS, rows, part), BF16),
            pltpu.VMEM((CHIPS, rows, part), BF16),
            pltpu.VMEM((rows, 2 * half), F32),
            pltpu.VMEM((rows, 2 * half), F32),
            pltpu.VMEM((rows, 128), F32),
            pltpu.VMEM((rows, 128), F32),
            pltpu.VMEM((text, width), BF16),
            pltpu.VMEM((2, text, tn), BF16),
            pltpu.VMEM((2, width, tn), BF16),
            pltpu.SemaphoreType.DMA((2, n_heads)),
            pltpu.SemaphoreType.DMA((2, n_heads)),
            pltpu.SemaphoreType.DMA((2, n_heads)),
            pltpu.SemaphoreType.DMA((CHIPS,)),
            pltpu.SemaphoreType.DMA((CHIPS,)),
            pltpu.SemaphoreType.DMA((CHIPS, n_heads)),
            pltpu.SemaphoreType.DMA((CHIPS, n_heads)),
            pltpu.SemaphoreType.DMA,
            pltpu.SemaphoreType.DMA((2,)),
            pltpu.SemaphoreType.DMA((2,)),
        ],
        compiler_params=pltpu.CompilerParams(vmem_limit_bytes=VMEM_LIMIT, collective_id=1, has_side_effects=True),
        cost_estimate=pl.CostEstimate(flops=flops, bytes_accessed=8 * half * part + 2 * width * width, transcendentals=2 * half * half * n_heads),
        name='attend',
    )(q, k, v, ctx, cwv)


def tail_kernel(te_ref, bm_ref, bo_ref, nw_ref, nb_ref, cgq_ref, x_hbm, o_ref, ck_ref, cv_ref, wo_ref, cwq_ref, cwo_ref, w1_ref, w2_ref,
                out_ref, a_ref, b_ref, xf_ref, h_ref, u_ref, ss_ref, mean_ref, vec_ref, mod_ref, kbuf, vbuf,
                s0_ref, s1_ref, s2_ref, s3_ref, g0_ref, g1_ref, stage_ref, ring_ref, ring_sem, in_sem, kv_sem, stage_sem):
    rows, width = xf_ref.shape
    ff = u_ref.shape[1]
    text = kbuf.shape[1]
    tn = ring_ref.shape[2]
    per = tn // 128
    nt = width // tn
    n_ff = ff // tn
    k_parts = 1
    while ff // k_parts > width or ff % k_parts:
        k_parts += 1
    kc = ff // k_parts
    part = width // CHIPS
    ring = Ring(ring_ref, ring_sem, [
        (nt, wo_ref, width, tn, 1, 0), (nt, cwq_ref, width, tn, 1, 0), (nt, cwo_ref, width, tn, 1, 0),
        (n_ff, w1_ref, width, tn, 1, 0), (nt * k_parts, w2_ref, kc, tn, k_parts, 0)])
    in_copies = [pltpu.make_async_copy(o_ref.at[d], a_ref.at[:, pl.ds(d * part, part)], in_sem) for d in range(CHIPS)]
    in_copies.append(pltpu.make_async_copy(x_hbm, b_ref, in_sem))
    for c in in_copies:
        c.start()
    ring.prime()
    load_vectors(vec_ref, (bo_ref, nw_ref, nb_ref, cgq_ref))
    BO, NW, NB, CGQ = range(4)
    mod_ref[...] = te_ref[...] + bm_ref[...]
    ss_ref[...] = jnp.zeros_like(ss_ref)
    for c in in_copies:
        c.wait()

    def vec(n, k):
        return vec_ref[n, pl.ds(k, 1), :]

    def mod(n, k):
        return mod_ref[n:n + 1, cols_of(k, 128)]

    def dots(phase, n, lhs, finish):
        def body(t, _):
            slots = [ring.wait(phase, 2 * t + i) for i in range(2)]
            for i in range(2):
                finish(2 * t + i, dot(lhs[...], ring_ref[slots[i]]))
            for i in range(2):
                ring.refill(phase, 2 * t + i)
            return 0

        lax.fori_loop(0, n // 2, body, 0)

    def o_done(i, acc):
        total = ss_ref[...]
        for g, a in enumerate(groups(acc)):
            k = i * per + g
            cols = cols_of(k, 128)
            x1 = b_ref[:, cols].astype(F32) + mod(G1, k) * (a + vec(BO, k))
            xf_ref[:, cols] = x1
            total = total + x1
        ss_ref[...] = total

    dots(0, nt, a_ref, o_done)

    def norm_to(dst, mul, add):
        def store(k, val):
            dst[:, cols_of(k, 128)] = val.astype(BF16)

        layer_norm(lambda k: xf_ref[:, cols_of(k, 128)], store, mul, add, rows, width, ss_ref, mean_ref, True)

    norm_to(b_ref, lambda k: vec(NW, k), lambda k: vec(NB, k))
    ss_ref[...] = jnp.zeros_like(ss_ref)

    def cq_done(i, acc):
        h_ref[:, cols_of(i, tn)] = acc
        add_lanes(ss_ref, rows, acc, True)

    dots(1, nt, b_ref, cq_done)
    rms_scale(ss_ref, rows, width)

    def cq_head(j, _):
        cols = cols_of(j, HEAD)
        a_ref[:, cols] = ((h_ref[:, cols] * ss_ref[...]) * vec(CGQ, j)).astype(BF16)
        return 0

    gw = kbuf.shape[2]
    n_groups = width // gw
    heads = gw // HEAD

    def kv_loads(g, slot):
        cols = cols_of(g, gw)
        return (pltpu.make_async_copy(ck_ref.at[:, cols], kbuf.at[slot], kv_sem.at[0, slot]),
                pltpu.make_async_copy(cv_ref.at[:, cols], vbuf.at[slot], kv_sem.at[1, slot]))

    for c in kv_loads(0, 0):
        c.start()
    lax.fori_loop(0, width // HEAD, cq_head, 0)
    s_refs = (s0_ref, s1_ref, s2_ref, s3_ref)

    def cross_group(g, _):
        slot = lax.rem(g, 2)
        for c in kv_loads(g, slot):
            c.wait()

        @pl.when(g + 1 < n_groups)
        def _():
            for c in kv_loads(g + 1, 1 - slot):
                c.start()

        tops = []

        def score(j):
            s = dot_nt(a_ref[:, cols_of(g * heads + j, HEAD)], kbuf[slot, :, j * HEAD:(j + 1) * HEAD])
            s_refs[j % 4][...] = s
            parts = groups(s)
            mx = parts[0]
            for p in parts[1:]:
                mx = jnp.maximum(mx, p)
            tops.append(jnp.broadcast_to(jnp.max(mx, axis=1, keepdims=True), (rows, 128)))

        def weigh(j):
            total = jnp.zeros((rows, 128), F32)
            parts = []
            for c in range(text // 128):
                p = jnp.exp2((s_refs[j % 4][:, c * 128:(c + 1) * 128] - tops[j]) * SM_C)
                total = total + p
                parts.append(p.astype(BF16))
            acc = dot(jnp.concatenate(parts, axis=1), vbuf[slot, :, j * HEAD:(j + 1) * HEAD])
            b_ref[:, cols_of(g * heads + j, HEAD)] = (acc / jnp.sum(total, axis=1, keepdims=True)).astype(BF16)

        score(0)
        for j in range(1, heads):
            score(j)
            weigh(j - 1)
        weigh(heads - 1)
        return 0

    lax.fori_loop(0, n_groups, cross_group, 0)
    ss_ref[...] = jnp.zeros_like(ss_ref)

    def co_done(i, acc):
        total = ss_ref[...]
        for g, a in enumerate(groups(acc)):
            cols = cols_of(i * per + g, 128)
            x2 = xf_ref[:, cols] + a
            xf_ref[:, cols] = x2
            total = total + x2
        ss_ref[...] = total

    dots(2, nt, b_ref, co_done)
    norm_to(a_ref, lambda k: 1.0 + mod(SC2, k), lambda k: mod(SH2, k))

    def f1_gelu(i, src, g):
        u_ref[:, cols_of(i * per + g, 128)] = jax.nn.gelu(src[:, g * 128:(g + 1) * 128], approximate=True).astype(BF16)

    def f1_dot(slot, dst, old, src):
        acc = None
        kp = width // per
        for g in range(per):
            term = dot(a_ref[:, g * kp:(g + 1) * kp], ring_ref[slot, g * kp:(g + 1) * kp, :])
            acc = term if acc is None else acc + term
            if src is not None:
                f1_gelu(old, src, g)
        dst[...] = acc

    f1_dot(ring.wait(3, 0), g0_ref, None, None)
    ring.refill(3, 0)

    def f1_pair(t, _):
        i = 2 * t + 1
        slots = [ring.wait(3, i), ring.wait(3, i + 1)]
        f1_dot(slots[0], g1_ref, i - 1, g0_ref)
        f1_dot(slots[1], g0_ref, i, g1_ref)
        ring.refill(3, i)
        ring.refill(3, i + 1)
        return 0

    lax.fori_loop(0, (n_ff - 1) // 2, f1_pair, 0)
    for g in range(per):
        f1_gelu(n_ff - 1, g0_ref, g)

    def stage_copy(i, slot):
        return pltpu.make_async_copy(stage_ref.at[slot], out_ref.at[:, cols_of(i, tn)], stage_sem.at[slot])

    def f2_tile(i, _):
        s = lax.rem(i, 2)
        slots = [ring.wait(4, i * k_parts + c) for c in range(k_parts)]

        @pl.when(i >= 2)
        def _():
            stage_copy(i, s).wait()

        acc = None
        for c in range(k_parts):
            term = dot(u_ref[:, c * kc:(c + 1) * kc], ring_ref[slots[c], 0:kc, :])
            acc = term if acc is None else acc + term
        for g, a in enumerate(groups(acc)):
            k = i * per + g
            stage_ref[s, :, g * 128:(g + 1) * 128] = (xf_ref[:, cols_of(k, 128)] + mod(G2, k) * a).astype(BF16)
        stage_copy(i, s).start()
        for c in range(k_parts):
            ring.refill(4, i * k_parts + c)
        return 0

    lax.fori_loop(0, nt, f2_tile, 0)
    for i in range(2):
        stage_copy(0, i).wait()


def tail_call(te, bm, vectors, x, o, ck, cv, wo, cwq, cwo, w1, w2, tn):
    rows, width = x.shape
    text = ck.shape[0]
    ff = w1.shape[1]
    flops = 2 * rows * width * (3 * width + 2 * ff) + 4 * rows * text * width
    assert (width // tn) % 2 == 0 and (ff // tn) % 2 == 1 and len(vectors) == 4
    return pl.pallas_call(
        tail_kernel,
        out_shape=jax.ShapeDtypeStruct((rows, width), BF16),
        in_specs=[vmem_spec()] * (2 + len(vectors)) + [any_spec()] * 9,
        out_specs=any_spec(),
        scratch_shapes=[
            pltpu.VMEM((rows, width), BF16),
            pltpu.VMEM((rows, width), BF16),
            pltpu.VMEM((rows, width), F32),
            pltpu.VMEM((rows, width), F32),
            pltpu.VMEM((rows, ff), BF16),
            pltpu.VMEM((rows, 128), F32),
            pltpu.VMEM((rows, 128), F32),
            pltpu.VMEM((len(vectors), width // 128, 128), F32),
            pltpu.VMEM(te.shape, F32),
            pltpu.VMEM((2, text, 8 * HEAD), BF16),
            pltpu.VMEM((2, text, 8 * HEAD), BF16),
            pltpu.VMEM((rows, text), F32),
            pltpu.VMEM((rows, text), F32),
            pltpu.VMEM((rows, text), F32),
            pltpu.VMEM((rows, text), F32),
            pltpu.VMEM((rows, tn), F32),
            pltpu.VMEM((rows, tn), F32),
            pltpu.VMEM((2, rows, tn), BF16),
            pltpu.VMEM((5, width, tn), BF16),
            pltpu.SemaphoreType.DMA((5,)),
            pltpu.SemaphoreType.DMA,
            pltpu.SemaphoreType.DMA((2, 2)),
            pltpu.SemaphoreType.DMA((2,)),
        ],
        compiler_params=pltpu.CompilerParams(vmem_limit_bytes=VMEM_LIMIT),
        cost_estimate=pl.CostEstimate(flops=flops, bytes_accessed=2 * width * (3 * width + 2 * ff), transcendentals=rows * ff),
        name='tail',
    )(te, bm, *vectors, x, o, ck, cv, wo, cwq, cwo, w1, w2)


def solution(mesh):
    tok_spec = P('dp', ('sp', 'uly'), None)
    batch_spec = P('dp', None, None)

    def local_block(tokens, rope_ang, t_emb, block_mod, context, attn_wq, attn_bq, attn_wk, attn_bk, attn_wv, attn_bv, attn_gq, attn_gk, attn_wo, attn_bo, norm3_w, norm3_b, cross_wq, cross_wk, cross_wv, cross_gq, cross_gk, cross_wo, ffn_w1, ffn_w2):
        x, te, bm, ctx = tokens[0], t_emb[0], block_mod[0], context[0]
        tn = min(512, x.shape[1] // CHIPS)

        def lanes(*vectors):
            return tuple(v.reshape(-1, 128) for v in vectors)

        q, k, v, ck = qkv_call(x, te, bm, rope_ang, lanes(attn_bq, attn_bk, attn_bv, attn_gq, attn_gk, cross_gk), ctx,
                               attn_wv, attn_wk, attn_wq, cross_wk, tn)
        o, cv = attend_call(q, k, v, ctx, cross_wv, tn)
        out = tail_call(te, bm, lanes(attn_bo, norm3_w, norm3_b, cross_gq), x, o, ck, cv, attn_wo, cross_wq, cross_wo, ffn_w1, ffn_w2, tn)
        return out[None]

    in_specs = (tok_spec, P(('sp', 'uly'), None), batch_spec, P(), batch_spec) + (P(),) * 20
    return jax.shard_map(local_block, mesh=mesh, in_specs=in_specs, out_specs=tok_spec, check_vma=False)
```

time: 488 us -> 473 us (0.969)
    pallas_call x1, Pallas kernels: 154 us -> 139 us  [qkv_call(): pl.pallas_call(qkv_kernel, out_shape=(split, gathered, gathered, jax.Shap...]
    another operation x11 -> x0, local copies, waits for them, and re-layouts: 7.48 us -> none  [local_block(): jnp.stack([attn_bq, attn_bk, attn_bv, attn_bo, attn_gq, attn_gk, norm3_w,...]
    pallas_call x1, Pallas kernels: 133 us -> 140 us  [attend_call(): pl.pallas_call(attend_kernel, out_shape=(jax.ShapeDtypeStruct((CHIPS, row...]
    pallas_call x1, Pallas kernels: 185 us -> 190 us  [tail_call(): pl.pallas_call(tail_kernel, out_shape=jax.ShapeDtypeStruct((rows, width),...]
where the time goes in v2:
time: 473 us
  Pallas kernels  469 us (99%)
    pallas_call x1, Pallas kernels, tail_call(): pl.pallas_call(tail_kernel, out_shape=jax.ShapeDtypeStruct((rows, width),...  190 us
    pallas_call x1, Pallas kernels, attend_call(): pl.pallas_call(attend_kernel, out_shape=(jax.ShapeDtypeStruct((CHIPS, row...  140 us
    pallas_call x1, Pallas kernels, qkv_call(): pl.pallas_call(qkv_kernel, out_shape=(split, gathered, gathered, jax.Shap...  139 us

profile of v2, /device:TPU:8, one launch (start us, length us, event | category | flops | bytes accessed | tf_op | source)
XLA Modules:
  0.0 472.9 jit_solution(8365001415821314076)
XLA Ops:
  0.0 1.7 copy.26.ang_ref
  1.7 1.8 copy_bitcast_fusion
  3.4 139.2 %qkv.1 = (bf16[8,288,640]{2,1,0:T(8,128)(2,1)}, bf16[2304,640]{1,0:T(8,128)(2,1)}, bf16[2304,640]{1,0:T(8,128)(2,1)}, bf16[512,5120]{1,0:T(8,128)(2,1)}) custom-call(bf16[288,5120]{1,0:T(8,128)(2,1)} %bitcast.19, f32[6,5120]{1,0:T(8,128)} %get-tuple-element.18.te_ref, f32[6,5120]{1,0:T(8,128)} %get-tuple-element.17.bm_ref, f32[288,64]{1,0:T(8,128)} %copy.26.ang_ref, ...), custom_call_target="tpu_custom_call" | custom-call | flops 72142028800 | bytes 209715200 | tf_op jit(solution)/shard_map/qkv/pallas_call | solution.py:343
  142.6 140.4 %attend.1 = (bf16[8,288,640]{2,1,0:T(8,128)(2,1)}, bf16[512,5120]{1,0:T(8,128)(2,1)}) custom-call(bf16[8,288,640]{2,1,0:T(8,128)(2,1)} %get-tuple-element.11.q_ref, bf16[2304,640]{1,0:T(8,128)(2,1)} %get-tuple-element.12.k_ref, bf16[2304,640]{1,0:T(8,128)(2,1)} %get-tuple-element.13.v_ref, bf16[512,5120]{1,0:T(8,128)(2,1)} %bitcast.18, ...), custom_call_target="tpu_custom_call" | custom-call | flops 54022635520 | bytes 64225280 | tf_op jit(solution)/shard_map/attend/pallas_call | solution.py:552
  283.1 189.6 %tail.1 = bf16[288,5120]{1,0:T(8,128)(2,1)} custom-call(f32[6,5120]{1,0:T(8,128)} %get-tuple-element.18.te_ref, f32[6,5120]{1,0:T(8,128)} %get-tuple-element.17.bm_ref, bf16[40,128]{1,0:T(8,128)(2,1)} %bitcast.27, bf16[40,128]{1,0:T(8,128)(2,1)} %bitcast.28, bf16[40,128]{1,0:T(8,128)(2,1)} %bitcast.29, bf16[40,128]{1,0:T(8,128)(2,1)} %bitcast.30, ...), custom_call_target="tpu_custom_call" | custom-call | flops 129855651840 | bytes 440401920 | tf_op jit(solution)/shard_map/tail/pallas_call | solution.py:796

commit v3 on v2

--- a/solution.py
+++ b/solution.py
@@ -55,8 +55,8 @@
 
 
 class Ring:
-    def __init__(self, slots, sems, phases):
-        self.slots, self.sems, self.phases = slots, sems, phases
+    def __init__(self, slots, sems, phases, queues=1):
+        self.slots, self.sems, self.phases, self.queues = slots, sems, phases, queues
         self.depth = slots.shape[0]
         self.base = [sum(p[0] for p in phases[:i]) for i in range(len(phases) + 1)]
 
@@ -76,8 +76,8 @@
         return out
 
     def start(self, phase, tile):
-        for c in self.copies(phase, tile):
-            c.start()
+        for n, c in enumerate(self.copies(phase, tile)):
+            c.start(priority=n % self.queues)
 
     def prime(self):
         for i in range(self.depth):
@@ -200,7 +200,7 @@
         y_ref[:, cols_of(k, 128)] = val.astype(BF16)
 
     layer_norm(lambda k: x_ref[:, cols_of(k, 128)].astype(F32), store_y,
-               lambda k: 1.0 + mod_ref[SC1:SC1 + 1, cols_of(k, 128)], lambda k: mod_ref[SH1:SH1 + 1, cols_of(k, 128)],
+               lambda k: 1.0 + mod_ref[SC1, pl.ds(k, 1), :], lambda k: mod_ref[SH1, pl.ds(k, 1), :],
                rows, width, ss_ref, mean_ref, False)
     pl.semaphore_wait(barrier, n_signals)
 
@@ -236,8 +236,8 @@
         for r in range(1, CHIPS // 2):
             remote(0, v_out, r).start()
         local(0, v_out).start()
+        lane = lax.broadcasted_iota(jnp.int32, (rows, HEAD), 1)
         ang = jnp.concatenate([ang_ref[...], ang_ref[...]], axis=1)
-        lane = lax.broadcasted_iota(jnp.int32, (rows, HEAD), 1)
         spread = jnp.take_along_axis(ang, lane // 2, axis=1)
         cos_ref[...] = jnp.cos(spread)
         sin_ref[...] = jnp.where(lax.rem(lane, 2) == 0, -1.0, 1.0) * jnp.sin(spread)
@@ -371,9 +371,9 @@
     )(x, te, bm, ang, *vectors, ctx, wv, wk, wq, cwk)
 
 
-def attend_kernel(q_ref, k_ref, v_ref, ctx_hbm, cwv_ref, o_out, cv_out,
-                  kbuf, vbuf, qbuf, obuf, s0_ref, s1_ref, mx0_ref, mx1_ref, ctx_ref, stage_ref, ring_ref,
-                  own_sem, pair_send, pair_recv, q_send, q_recv, o_send, o_recv, ctx_sem, stage_sem, ring_sem):
+def attend_kernel(te_ref, bm_ref, bo_ref, q_ref, k_ref, v_ref, ctx_hbm, cwv_ref, x_hbm, wo_ref, x1_out, cv_out,
+                  kbuf, vbuf, qbuf, obuf, s0_ref, s1_ref, mx0_ref, mx1_ref, ctx_ref, stage_ref, ring_ref, acc_ref, wo_ring, row_ref,
+                  own_sem, pair_send, pair_recv, q_send, q_recv, o_send, o_recv, ctx_sem, stage_sem, ring_sem, wo_sem):
     n_heads, keys, _ = kbuf.shape
     half = keys // 2
     rows = qbuf.shape[1]
@@ -402,14 +402,10 @@
             src_ref=q_ref.at[to], dst_ref=qbuf.at[r], send_sem=q_send.at[r], recv_sem=q_recv.at[r],
             device_id=device_at(to, core), device_id_type=MESH)
 
-    def o_local(h):
-        cols = cols_of(h, HEAD)
-        return pltpu.make_async_copy(obuf.at[0, :, cols], o_out.at[me, :, cols], o_send.at[0, h])
-
     def o_remote(r, h):
         cols = cols_of(h, HEAD)
         return pltpu.make_async_remote_copy(
-            src_ref=obuf.at[r, :, cols], dst_ref=o_out.at[me, :, cols], send_sem=o_send.at[r, h], recv_sem=o_recv.at[r, h],
+            src_ref=qbuf.at[r, :, cols], dst_ref=obuf.at[r, :, cols], send_sem=o_send.at[r, h], recv_sem=o_recv.at[r, h],
             device_id=device_at(flip(me, r), core), device_id_type=MESH)
 
     q_local().start()
@@ -434,6 +430,13 @@
     def stage_copy(i, slot):
         return pltpu.make_async_copy(stage_ref.at[slot], cv_out.at[:, cols_of(i, tn)], stage_sem.at[slot])
 
+    def wo_copy(r, side):
+        return pltpu.make_async_copy(wo_ref.at[cols_of(flip(me, r), wo_ring.shape[1]), pl.ds(side * wo_ring.shape[2], wo_ring.shape[2])],
+                                     wo_ring.at[side], wo_sem.at[side])
+
+    for side in range(2):
+        wo_copy(0, side).start()
+
     def cv_tile(i):
         slot = ring.wait(0, i)
         s = lax.rem(i, 2)
@@ -452,10 +455,6 @@
 
     def send_output(b):
         r, h = b // n_heads, lax.rem(b, n_heads)
-
-        @pl.when(r == 0)
-        def _():
-            o_local(h).start()
 
         @pl.when(r > 0)
         def _():
@@ -508,7 +507,7 @@
                 acc = acc + dot(jnp.concatenate(parts, axis=1), vbuf[old_h, j * kb:(j + 1) * kb, :])
         mx_now[...] = jnp.broadcast_to(jnp.max(mx, axis=1, keepdims=True), (rows, 128))
         if before is not None:
-            obuf[old_r, :, cols_of(old_h, HEAD)] = (acc / jnp.sum(total, axis=1, keepdims=True)).astype(BF16)
+            qbuf[old_r, :, cols_of(old_h, HEAD)] = (acc / jnp.sum(total, axis=1, keepdims=True)).astype(BF16)
 
     bufs = ((s0_ref, mx0_ref), (s1_ref, mx1_ref))
     step(jnp.int32(0), bufs[0], None)
@@ -528,31 +527,83 @@
     send_output(jnp.int32(blocks - 1))
     for i in range(2):
         stage_copy(0, i).wait()
-
+    width = acc_ref.shape[1]
+    part = qbuf.shape[2]
+    half_n = width // 2
+    x_copy = pltpu.make_async_copy(x_hbm, ctx_ref.at[0:rows], ctx_sem)
+    x_copy.start()
+    row_ref[0] = te_ref[G1] + bm_ref[G1]
+    row_ref[1] = bo_ref[...].astype(F32)
+
+    def project(r, lhs, side, finish):
+        wo_copy(r, side).wait()
+        for n in range(half_n // tn):
+            cols = pl.ds(side * half_n + n * tn, tn)
+            finish(cols, side * half_n + n * tn, dot(lhs[...], wo_ring[side, :, n * tn:(n + 1) * tn]))
+
+    def first(cols, c0, prod):
+        acc_ref[:, cols] = prod
+
+    def middle(cols, c0, prod):
+        acc_ref[:, cols] = acc_ref[:, cols] + prod
+
+    def last(cols, c0, prod):
+        for g, p in enumerate(groups(prod)):
+            k = c0 // 128 + g
+            gc = slice(c0 + g * 128, c0 + (g + 1) * 128)
+            acc_ref[:, gc] = ctx_ref[0:rows, gc].astype(F32) + row_ref[0, k:k + 1, :] * (acc_ref[:, gc] + p + row_ref[1, k:k + 1, :])
+
+    def arrived(r):
+        for h in range(n_heads):
+            o_remote(r, h).wait_recv()
+
+    def x1_copy(side):
+        cols = pl.ds(side * half_n, half_n)
+        return pltpu.make_async_copy(acc_ref.at[:, cols], x1_out.at[:, cols], stage_sem.at[side])
+
+    for side in range(2):
+        project(0, qbuf.at[0], side, first)
+        wo_copy(1, side).start()
+
+    def chunk(r, _):
+        arrived(r)
+        for side in range(2):
+            project(r, obuf.at[r], side, middle)
+            wo_copy(r + 1, side).start()
+        return 0
+
+    lax.fori_loop(1, CHIPS - 1, chunk, 0)
+    x_copy.wait()
+    arrived(CHIPS - 1)
+    project(CHIPS - 1, obuf.at[CHIPS - 1], 0, last)
+    project(CHIPS - 1, obuf.at[CHIPS - 1], 1, last)
+    x1_copy(0).start()
     for h in range(n_heads):
         for c in pair(h):
             c.wait_send()
-        o_local(h).wait()
 
     def drain(r, _):
         q_remote(r).wait_send()
         for h in range(n_heads):
-            o_remote(r, h).wait()
+            o_remote(r, h).wait_send()
         return 0
 
     lax.fori_loop(1, CHIPS, drain, 0)
-
-
-def attend_call(q, k, v, ctx, cwv, tn):
+    x1_copy(1).start()
+    for side in range(2):
+        x1_copy(side).wait()
+
+
+def attend_call(te, bm, bo, q, k, v, ctx, cwv, x, wo, tn):
     _, rows, part = q.shape
     half = k.shape[0]
     n_heads = part // HEAD
     text, width = ctx.shape
-    flops = 8 * half * half * part + 2 * text * width * width
+    flops = 8 * half * half * part + 2 * (text + rows) * width * width
     return pl.pallas_call(
         attend_kernel,
-        out_shape=(jax.ShapeDtypeStruct((CHIPS, rows, part), BF16), jax.ShapeDtypeStruct((text, width), BF16)),
-        in_specs=[any_spec()] * 5,
+        out_shape=(jax.ShapeDtypeStruct((rows, width), F32), jax.ShapeDtypeStruct((text, width), BF16)),
+        in_specs=[vmem_spec()] * 3 + [any_spec()] * 7,
         out_specs=[any_spec()] * 2,
         scratch_shapes=[
             pltpu.VMEM((n_heads, 2 * half, HEAD), BF16),
@@ -566,6 +617,9 @@
             pltpu.VMEM((text, width), BF16),
             pltpu.VMEM((2, text, tn), BF16),
             pltpu.VMEM((2, width, tn), BF16),
+            pltpu.VMEM((rows, width), F32),
+            pltpu.VMEM((2, part, width // 2), BF16),
+            pltpu.VMEM((2, width // 128, 128), F32),
             pltpu.SemaphoreType.DMA((2, n_heads)),
             pltpu.SemaphoreType.DMA((2, n_heads)),
             pltpu.SemaphoreType.DMA((2, n_heads)),
@@ -576,14 +630,15 @@
             pltpu.SemaphoreType.DMA,
             pltpu.SemaphoreType.DMA((2,)),
             pltpu.SemaphoreType.DMA((2,)),
+            pltpu.SemaphoreType.DMA((2,)),
         ],
         compiler_params=pltpu.CompilerParams(vmem_limit_bytes=VMEM_LIMIT, collective_id=1, has_side_effects=True),
-        cost_estimate=pl.CostEstimate(flops=flops, bytes_accessed=8 * half * part + 2 * width * width, transcendentals=2 * half * half * n_heads),
+        cost_estimate=pl.CostEstimate(flops=flops, bytes_accessed=8 * half * part + 4 * width * width, transcendentals=2 * half * half * n_heads),
         name='attend',
-    )(q, k, v, ctx, cwv)
-
-
-def tail_kernel(te_ref, bm_ref, bo_ref, nw_ref, nb_ref, cgq_ref, x_hbm, o_ref, ck_ref, cv_ref, wo_ref, cwq_ref, cwo_ref, w1_ref, w2_ref,
+    )(te, bm, bo, q, k, v, ctx, cwv, x, wo)
+
+
+def tail_kernel(te_ref, bm_ref, nw_ref, nb_ref, cgq_ref, x1_ref, ck_ref, cv_ref, cwq_ref, cwo_ref, w1_ref, w2_ref,
                 out_ref, a_ref, b_ref, xf_ref, h_ref, u_ref, ss_ref, mean_ref, vec_ref, mod_ref, kbuf, vbuf,
                 s0_ref, s1_ref, s2_ref, s3_ref, g0_ref, g1_ref, stage_ref, ring_ref, ring_sem, in_sem, kv_sem, stage_sem):
     rows, width = xf_ref.shape
@@ -597,27 +652,22 @@
     while ff // k_parts > width or ff % k_parts:
         k_parts += 1
     kc = ff // k_parts
-    part = width // CHIPS
     ring = Ring(ring_ref, ring_sem, [
-        (nt, wo_ref, width, tn, 1, 0), (nt, cwq_ref, width, tn, 1, 0), (nt, cwo_ref, width, tn, 1, 0),
-        (n_ff, w1_ref, width, tn, 1, 0), (nt * k_parts, w2_ref, kc, tn, k_parts, 0)])
-    in_copies = [pltpu.make_async_copy(o_ref.at[d], a_ref.at[:, pl.ds(d * part, part)], in_sem) for d in range(CHIPS)]
-    in_copies.append(pltpu.make_async_copy(x_hbm, b_ref, in_sem))
-    for c in in_copies:
-        c.start()
+        (nt, cwq_ref, width, tn, 1, 0), (nt, cwo_ref, width, tn, 1, 0),
+        (n_ff, w1_ref, width, tn, 1, 0), (nt * k_parts, w2_ref, kc, tn, k_parts, 0)], 2)
+    x1_copy = pltpu.make_async_copy(x1_ref, xf_ref, in_sem)
+    x1_copy.start()
     ring.prime()
-    load_vectors(vec_ref, (bo_ref, nw_ref, nb_ref, cgq_ref))
-    BO, NW, NB, CGQ = range(4)
+    load_vectors(vec_ref, (nw_ref, nb_ref, cgq_ref))
+    NW, NB, CGQ = range(3)
     mod_ref[...] = te_ref[...] + bm_ref[...]
-    ss_ref[...] = jnp.zeros_like(ss_ref)
-    for c in in_copies:
-        c.wait()
+    x1_copy.wait()
 
     def vec(n, k):
         return vec_ref[n, pl.ds(k, 1), :]
 
     def mod(n, k):
-        return mod_ref[n:n + 1, cols_of(k, 128)]
+        return mod_ref[n, pl.ds(k, 1), :]
 
     def dots(phase, n, lhs, finish):
         def body(t, _):
@@ -630,32 +680,20 @@
 
         lax.fori_loop(0, n // 2, body, 0)
 
-    def o_done(i, acc):
-        total = ss_ref[...]
-        for g, a in enumerate(groups(acc)):
-            k = i * per + g
-            cols = cols_of(k, 128)
-            x1 = b_ref[:, cols].astype(F32) + mod(G1, k) * (a + vec(BO, k))
-            xf_ref[:, cols] = x1
-            total = total + x1
-        ss_ref[...] = total
-
-    dots(0, nt, a_ref, o_done)
-
-    def norm_to(dst, mul, add):
+    def norm_to(dst, mul, add, have_sum):
         def store(k, val):
             dst[:, cols_of(k, 128)] = val.astype(BF16)
 
-        layer_norm(lambda k: xf_ref[:, cols_of(k, 128)], store, mul, add, rows, width, ss_ref, mean_ref, True)
-
-    norm_to(b_ref, lambda k: vec(NW, k), lambda k: vec(NB, k))
+        layer_norm(lambda k: xf_ref[:, cols_of(k, 128)], store, mul, add, rows, width, ss_ref, mean_ref, have_sum)
+
+    norm_to(b_ref, lambda k: vec(NW, k), lambda k: vec(NB, k), False)
     ss_ref[...] = jnp.zeros_like(ss_ref)
 
     def cq_done(i, acc):
         h_ref[:, cols_of(i, tn)] = acc
         add_lanes(ss_ref, rows, acc, True)
 
-    dots(1, nt, b_ref, cq_done)
+    dots(0, nt, b_ref, cq_done)
     rms_scale(ss_ref, rows, width)
 
     def cq_head(j, _):
@@ -727,8 +765,8 @@
             total = total + x2
         ss_ref[...] = total
 
-    dots(2, nt, b_ref, co_done)
-    norm_to(a_ref, lambda k: 1.0 + mod(SC2, k), lambda k: mod(SH2, k))
+    dots(1, nt, b_ref, co_done)
+    norm_to(a_ref, lambda k: 1.0 + mod(SC2, k), lambda k: mod(SH2, k), True)
 
     def f1_gelu(i, src, g):
         u_ref[:, cols_of(i * per + g, 128)] = jax.nn.gelu(src[:, g * 128:(g + 1) * 128], approximate=True).astype(BF16)
@@ -743,16 +781,16 @@
                 f1_gelu(old, src, g)
         dst[...] = acc
 
-    f1_dot(ring.wait(3, 0), g0_ref, None, None)
-    ring.refill(3, 0)
+    f1_dot(ring.wait(2, 0), g0_ref, None, None)
+    ring.refill(2, 0)
 
     def f1_pair(t, _):
         i = 2 * t + 1
-        slots = [ring.wait(3, i), ring.wait(3, i + 1)]
+        slots = [ring.wait(2, i), ring.wait(2, i + 1)]
         f1_dot(slots[0], g1_ref, i - 1, g0_ref)
         f1_dot(slots[1], g0_ref, i, g1_ref)
-        ring.refill(3, i)
-        ring.refill(3, i + 1)
+        ring.refill(2, i)
+        ring.refill(2, i + 1)
         return 0
 
     lax.fori_loop(0, (n_ff - 1) // 2, f1_pair, 0)
@@ -764,7 +802,7 @@
 
     def f2_tile(i, _):
         s = lax.rem(i, 2)
-        slots = [ring.wait(4, i * k_parts + c) for c in range(k_parts)]
+        slots = [ring.wait(3, i * k_parts + c) for c in range(k_parts)]
 
         @pl.when(i >= 2)
         def _():
@@ -779,7 +817,7 @@
             stage_ref[s, :, g * 128:(g + 1) * 128] = (xf_ref[:, cols_of(k, 128)] + mod(G2, k) * a).astype(BF16)
         stage_copy(i, s).start()
         for c in range(k_parts):
-            ring.refill(4, i * k_parts + c)
+            ring.refill(3, i * k_parts + c)
         return 0
 
     lax.fori_loop(0, nt, f2_tile, 0)
@@ -787,16 +825,16 @@
         stage_copy(0, i).wait()
 
 
-def tail_call(te, bm, vectors, x, o, ck, cv, wo, cwq, cwo, w1, w2, tn):
-    rows, width = x.shape
+def tail_call(te, bm, vectors, x1, ck, cv, cwq, cwo, w1, w2, tn):
+    rows, width = x1.shape
     text = ck.shape[0]
     ff = w1.shape[1]
-    flops = 2 * rows * width * (3 * width + 2 * ff) + 4 * rows * text * width
-    assert (width // tn) % 2 == 0 and (ff // tn) % 2 == 1 and len(vectors) == 4
+    flops = 2 * rows * width * (2 * width + 2 * ff) + 4 * rows * text * width
+    assert (width // tn) % 2 == 0 and (ff // tn) % 2 == 1 and len(vectors) == 3
     return pl.pallas_call(
         tail_kernel,
         out_shape=jax.ShapeDtypeStruct((rows, width), BF16),
-        in_specs=[vmem_spec()] * (2 + len(vectors)) + [any_spec()] * 9,
+        in_specs=[vmem_spec()] * (2 + len(vectors)) + [any_spec()] * 7,
         out_specs=any_spec(),
         scratch_shapes=[
             pltpu.VMEM((rows, width), BF16),
@@ -824,9 +862,9 @@
             pltpu.SemaphoreType.DMA((2,)),
         ],
         compiler_params=pltpu.CompilerParams(vmem_limit_bytes=VMEM_LIMIT),
-        cost_estimate=pl.CostEstimate(flops=flops, bytes_accessed=2 * width * (3 * width + 2 * ff), transcendentals=rows * ff),
+        cost_estimate=pl.CostEstimate(flops=flops, bytes_accessed=2 * width * (2 * width + 2 * ff), transcendentals=rows * ff),
         name='tail',
-    )(te, bm, *vectors, x, o, ck, cv, wo, cwq, cwo, w1, w2)
+    )(te, bm, *vectors, x1, ck, cv, cwq, cwo, w1, w2)
 
 
 def solution(mesh):
@@ -834,7 +872,8 @@
     batch_spec = P('dp', None, None)
 
     def local_block(tokens, rope_ang, t_emb, block_mod, context, attn_wq, attn_bq, attn_wk, attn_bk, attn_wv, attn_bv, attn_gq, attn_gk, attn_wo, attn_bo, norm3_w, norm3_b, cross_wq, cross_wk, cross_wv, cross_gq, cross_gk, cross_wo, ffn_w1, ffn_w2):
-        x, te, bm, ctx = tokens[0], t_emb[0], block_mod[0], context[0]
+        x, ctx = tokens[0], context[0]
+        te, bm = (m.reshape(6, -1, 128) for m in (t_emb, block_mod))
         tn = min(512, x.shape[1] // CHIPS)
 
         def lanes(*vectors):
@@ -842,8 +881,8 @@
 
         q, k, v, ck = qkv_call(x, te, bm, rope_ang, lanes(attn_bq, attn_bk, attn_bv, attn_gq, attn_gk, cross_gk), ctx,
                                attn_wv, attn_wk, attn_wq, cross_wk, tn)
-        o, cv = attend_call(q, k, v, ctx, cross_wv, tn)
-        out = tail_call(te, bm, lanes(attn_bo, norm3_w, norm3_b, cross_gq), x, o, ck, cv, attn_wo, cross_wq, cross_wo, ffn_w1, ffn_w2, tn)
+        x1, cv = attend_call(te, bm, *lanes(attn_bo), q, k, v, ctx, cross_wv, x, attn_wo, tn)
+        out = tail_call(te, bm, lanes(norm3_w, norm3_b, cross_gq), x1, ck, cv, cross_wq, cross_wo, ffn_w1, ffn_w2, tn)
         return out[None]
 
     in_specs = (tok_spec, P(('sp', 'uly'), None), batch_spec, P(), batch_spec) + (P(),) * 20

time: 473 us -> 472 us (level)
    pallas_call x1, Pallas kernels: 190 us -> 184 us  [tail_call(): pl.pallas_call(tail_kernel, out_shape=jax.ShapeDtypeStruct((rows, width),...]
    pallas_call x1, Pallas kernels: 140 us -> 146 us  [attend_call(): pl.pallas_call(attend_kernel, out_shape=(jax.ShapeDtypeStruct((rows, widt...]
where the time goes in v3:
time: 472 us; the launch traced here: 471 us
  Pallas kernels  469 us (99%)
    pallas_call x1, Pallas kernels, tail_call(): pl.pallas_call(tail_kernel, out_shape=jax.ShapeDtypeStruct((rows, width),...  184 us
    pallas_call x1, Pallas kernels, attend_call(): pl.pallas_call(attend_kernel, out_shape=(jax.ShapeDtypeStruct((rows, widt...  146 us
    pallas_call x1, Pallas kernels, qkv_call(): pl.pallas_call(qkv_kernel, out_shape=(split, gathered, gathered, jax.Shap...  139 us

profile of v3, /device:TPU:8, one launch (start us, length us, event | category | flops | bytes accessed | tf_op | source)
XLA Modules:
  0.0 471.0 jit_solution(2894322587481371625)
XLA Ops:
  0.0 1.7 copy.26.ang_ref
  1.7 139.2 %qkv.1 = (bf16[8,288,640]{2,1,0:T(8,128)(2,1)}, bf16[2304,640]{1,0:T(8,128)(2,1)}, bf16[2304,640]{1,0:T(8,128)(2,1)}, bf16[512,5120]{1,0:T(8,128)(2,1)}) custom-call(bf16[288,5120]{1,0:T(8,128)(2,1)} %bitcast.17, f32[6,40,128]{2,1,0:T(8,128)} %bitcast.19, f32[6,40,128]{2,1,0:T(8,128)} %bitcast.22, f32[288,64]{1,0:T(8,128)} %copy.26.ang_ref, ...), custom_call_target="tpu_custom_call" | custom-call | flops 72142028800 | bytes 209715200 | tf_op jit(solution)/shard_map/qkv/pallas_call | solution.py:343
  140.9 146.3 %attend.1 = (f32[288,5120]{1,0:T(8,128)}, bf16[512,5120]{1,0:T(8,128)(2,1)}) custom-call(f32[6,40,128]{2,1,0:T(8,128)} %bitcast.20, f32[6,40,128]{2,1,0:T(8,128)} %bitcast.23, bf16[40,128]{1,0:T(8,128)(2,1)} %bitcast.31, bf16[8,288,640]{2,1,0:T(8,128)(2,1)} %get-tuple-element.11.q_ref, bf16[2304,640]{1,0:T(8,128)(2,1)} %get-tuple-element.12.k_ref, ...), custom_call_target="tpu_custom_call" | custom-call | flops 69122129920 | bytes 116654080 | tf_op jit(solution)/shard_map/attend/pallas_call | solution.py:603
  287.2 183.7 %tail.1 = bf16[288,5120]{1,0:T(8,128)(2,1)} custom-call(f32[6,40,128]{2,1,0:T(8,128)} %bitcast.21, f32[6,40,128]{2,1,0:T(8,128)} %bitcast.24, bf16[40,128]{1,0:T(8,128)(2,1)} %bitcast.32, bf16[40,128]{1,0:T(8,128)(2,1)} %bitcast.33, bf16[40,128]{1,0:T(8,128)(2,1)} %bitcast.34, f32[288,5120]{1,0:T(8,128)} %get-tuple-element.14.x1_ref, ...), custom_call_target="tpu_custom_call" | custom-call | flops 114756157440 | bytes 387973120 | tf_op jit(solution)/shard_map/tail/pallas_call | solution.py:834

commit v4 on v3

--- a/solution.py
+++ b/solution.py
@@ -55,8 +55,8 @@
 
 
 class Ring:
-    def __init__(self, slots, sems, phases, queues=1):
-        self.slots, self.sems, self.phases, self.queues = slots, sems, phases, queues
+    def __init__(self, slots, sems, phases):
+        self.slots, self.sems, self.phases = slots, sems, phases
         self.depth = slots.shape[0]
         self.base = [sum(p[0] for p in phases[:i]) for i in range(len(phases) + 1)]
 
@@ -64,9 +64,9 @@
         return lax.rem(self.base[phase] + tile, self.depth)
 
     def copies(self, phase, tile):
-        n, w_ref, k_rows, n_cols, k_parts, shift = self.phases[phase]
+        n, w_ref, k_rows, n_cols, k_parts, shift, col0 = self.phases[phase]
         slot = self.slot(phase, tile)
-        cols = cols_of(lax.rem(tile // k_parts + shift, n // k_parts), n_cols)
+        cols = cols_of(col0 + lax.rem(tile // k_parts + shift, n // k_parts), n_cols)
         row0 = lax.rem(tile, k_parts) * k_rows
         quarter = k_rows // 4
         out = []
@@ -76,8 +76,8 @@
         return out
 
     def start(self, phase, tile):
-        for n, c in enumerate(self.copies(phase, tile)):
-            c.start(priority=n % self.queues)
+        for c in self.copies(phase, tile):
+            c.start()
 
     def prime(self):
         for i in range(self.depth):
@@ -171,8 +171,8 @@
 
 
 def qkv_kernel(x_ref, te_ref, bm_ref, ang_ref, bq_ref, bk_ref, bv_ref, gq_ref, gk_ref, cgk_ref,
-               ctx_hbm, wv_ref, wk_ref, wq_ref, cwk_ref,
-               q_out, k_out, v_out, ck_out,
+               ctx_hbm, wv_ref, wk_ref, wq_ref, cwk_ref, cwv_ref,
+               q_out, k_out, v_out, ck_out, cv_out,
                y_ref, h_ref, ss_ref, mean_ref, cos_ref, sin_ref, vec_ref, mod_ref, qkv_ref, ctx_ref, stage_ref, ring_ref,
                ring_sem, out_sem, ctx_sem, stage_sem, send_sem, recv_sem):
     rows, width = x_ref.shape
@@ -181,11 +181,13 @@
     per = tn // 128
     nt = width // tn
     part = width // CHIPS
+    n_cv = cv_out.shape[1] // tn
     me, core = my_place()
     barrier, n_signals = meet(me, core, False)
     far = (CHIPS // 2) * (1 - me // (CHIPS // 2))
     shift = far * part // tn
-    ring = Ring(ring_ref, ring_sem, [(nt, w, width, tn, 1, sh) for w, sh in ((wv_ref, shift), (wk_ref, 0), (wq_ref, 0), (cwk_ref, 0))])
+    ring = Ring(ring_ref, ring_sem, [(nt, w, width, tn, 1, sh, 0) for w, sh in ((wv_ref, shift), (wk_ref, 0), (wq_ref, 0), (cwk_ref, 0))]
+                + [(n_cv, cwv_ref, width, tn, 1, 0, 0)])
     ring.prime()
     ctx_copy = pltpu.make_async_copy(ctx_hbm, ctx_ref, ctx_sem)
     ctx_copy.start()
@@ -315,6 +317,19 @@
         return 0
 
     lax.fori_loop(0, nt, ck_norm, 0)
+    def cv_copy(i, slot):
+        return pltpu.make_async_copy(stage_ref.at[slot], cv_out.at[:, cols_of(i, tn)], stage_sem.at[slot])
+
+    def cv_tile(i, _):
+        slot = ring.wait(4, i)
+        s = lax.rem(nt + i, 2)
+        cv_copy(i, s).wait()
+        stage_ref[s] = dot(ctx_ref[...], ring_ref[slot]).astype(BF16)
+        cv_copy(i, s).start()
+        ring.refill(4, i)
+        return 0
+
+    lax.fori_loop(0, n_cv, cv_tile, 0)
     for i in range(2):
         stage_copy(0, i).wait()
     for c in q_copies():
@@ -333,18 +348,18 @@
     return pl.BlockSpec(memory_space=pltpu.VMEM)
 
 
-def qkv_call(x, te, bm, ang, vectors, ctx, wv, wk, wq, cwk, tn):
+def qkv_call(x, te, bm, ang, vectors, ctx, wv, wk, wq, cwk, cwv, cv_cols, tn):
     rows, width = x.shape
     text = ctx.shape[0]
     part = width // CHIPS
     split = jax.ShapeDtypeStruct((CHIPS, rows, part), BF16)
     gathered = jax.ShapeDtypeStruct((CHIPS * rows, part), BF16)
-    flops = 2 * width * width * (3 * rows + text)
+    flops = 2 * width * (width * (3 * rows + text) + cv_cols * text)
     return pl.pallas_call(
         qkv_kernel,
-        out_shape=(split, gathered, gathered, jax.ShapeDtypeStruct((text, width), BF16)),
-        in_specs=[vmem_spec()] * (4 + len(vectors)) + [any_spec()] * 5,
-        out_specs=[any_spec()] * 4,
+        out_shape=(split, gathered, gathered, jax.ShapeDtypeStruct((text, width), BF16), jax.ShapeDtypeStruct((text, cv_cols), BF16)),
+        in_specs=[vmem_spec()] * (4 + len(vectors)) + [any_spec()] * 6,
+        out_specs=[any_spec()] * 5,
         scratch_shapes=[
             pltpu.VMEM((rows, width), BF16),
             pltpu.VMEM((text, width), F32),
@@ -368,7 +383,7 @@
         compiler_params=pltpu.CompilerParams(vmem_limit_bytes=VMEM_LIMIT, collective_id=0, has_side_effects=True),
         cost_estimate=pl.CostEstimate(flops=flops, bytes_accessed=8 * width * width, transcendentals=0),
         name='qkv',
-    )(x, te, bm, ang, *vectors, ctx, wv, wk, wq, cwk)
+    )(x, te, bm, ang, *vectors, ctx, wv, wk, wq, cwk, cwv)
 
 
 def attend_kernel(te_ref, bm_ref, bo_ref, q_ref, k_ref, v_ref, ctx_hbm, cwv_ref, x_hbm, wo_ref, x1_out, cv_out,
@@ -422,7 +437,8 @@
             c.start()
     tn = ring_ref.shape[2]
     nt = ring_ref.shape[1] // tn
-    ring = Ring(ring_ref, ring_sem, [(nt, cwv_ref, ring_ref.shape[1], tn, 1, 0)])
+    n_cv = cv_out.shape[1] // tn
+    ring = Ring(ring_ref, ring_sem, [(n_cv, cwv_ref, ring_ref.shape[1], tn, 1, 0, nt - n_cv)])
     ring.prime()
     ctx_copy = pltpu.make_async_copy(ctx_hbm, ctx_ref, ctx_sem)
     ctx_copy.start()
@@ -516,13 +532,13 @@
         step(2 * t + 1, bufs[1], bufs[0])
         step(2 * t + 2, bufs[0], bufs[1])
 
-        @pl.when((lax.rem(t, every) == 0) & (t < nt * every))
+        @pl.when((lax.rem(t, every) == 0) & (t < n_cv * every))
         def _():
             cv_tile(t // every)
 
         return 0
 
-    every = blocks // 2 // nt
+    every = max(1, blocks // 2 // n_cv)
     lax.fori_loop(0, blocks // 2, pair_of_steps, 0)
     send_output(jnp.int32(blocks - 1))
     for i in range(2):
@@ -594,15 +610,15 @@
         x1_copy(side).wait()
 
 
-def attend_call(te, bm, bo, q, k, v, ctx, cwv, x, wo, tn):
+def attend_call(te, bm, bo, q, k, v, ctx, cwv, x, wo, cv_cols, tn):
     _, rows, part = q.shape
     half = k.shape[0]
     n_heads = part // HEAD
     text, width = ctx.shape
-    flops = 8 * half * half * part + 2 * (text + rows) * width * width
+    flops = 8 * half * half * part + 2 * width * (text * cv_cols + rows * width)
     return pl.pallas_call(
         attend_kernel,
-        out_shape=(jax.ShapeDtypeStruct((rows, width), F32), jax.ShapeDtypeStruct((text, width), BF16)),
+        out_shape=(jax.ShapeDtypeStruct((rows, width), F32), jax.ShapeDtypeStruct((text, cv_cols), BF16)),
         in_specs=[vmem_spec()] * 3 + [any_spec()] * 7,
         out_specs=[any_spec()] * 2,
         scratch_shapes=[
@@ -638,30 +654,72 @@
     )(te, bm, bo, q, k, v, ctx, cwv, x, wo)
 
 
-def tail_kernel(te_ref, bm_ref, nw_ref, nb_ref, cgq_ref, x1_ref, ck_ref, cv_ref, cwq_ref, cwo_ref, w1_ref, w2_ref,
+class Slabs:
+    def __init__(self, slots, sems, phases):
+        self.slots, self.sems, self.phases = slots, sems, phases
+        self.depth, self.rows = slots.shape[0], slots.shape[1]
+        self.base = [sum(p[0] for p in phases[:i]) for i in range(len(phases) + 1)]
+
+    def copies(self, phase, i):
+        n, w_ref, n_k, n_cols = self.phases[phase]
+        slot = lax.rem(self.base[phase] + i, self.depth)
+        cols = cols_of(i // n_k, n_cols)
+        quarter = self.rows // 4
+        return [pltpu.make_async_copy(w_ref.at[cols_of(lax.rem(i, n_k) * 4 + c, quarter), cols],
+                                      self.slots.at[slot, pl.ds(c * quarter, quarter), pl.ds(0, n_cols)], self.sems.at[slot]) for c in range(4)]
+
+    def start(self, phase, i):
+        for c in self.copies(phase, i):
+            c.start()
+
+    def prime(self):
+        for i in range(self.depth):
+            self.start(0, i)
+
+    def add_product(self, phase, i, lhs, k, acc_ref):
+        n, _, _, n_cols = self.phases[phase]
+        for c in self.copies(phase, i):
+            c.wait()
+        slot = lax.rem(self.base[phase] + i, self.depth)
+        per = self.rows // 128
+        left = jnp.concatenate([lhs[k * per + g] for g in range(per)], axis=1)
+        c0 = 0
+        while c0 < n_cols:
+            cols = slice(c0, min(c0 + 512, n_cols))
+            acc_ref[:, cols] = acc_ref[:, cols] + dot(left, self.slots[slot, :, cols])
+            c0 += 512
+        ahead = i + self.depth
+
+        @pl.when(ahead < n)
+        def _():
+            self.start(phase, ahead)
+
+        if phase + 1 < len(self.phases):
+            @pl.when(ahead >= n)
+            def _():
+                self.start(phase + 1, ahead - n)
+
+
+def tail_kernel(te_ref, bm_ref, nw_ref, nb_ref, cgq_ref, x1_ref, ck_ref, cva_ref, cvb_ref, cwq_ref, cwo_ref, w1_ref, w2_ref,
                 out_ref, a_ref, b_ref, xf_ref, h_ref, u_ref, ss_ref, mean_ref, vec_ref, mod_ref, kbuf, vbuf,
-                s0_ref, s1_ref, s2_ref, s3_ref, g0_ref, g1_ref, stage_ref, ring_ref, ring_sem, in_sem, kv_sem, stage_sem):
+                s0_ref, s1_ref, s2_ref, s3_ref, stage_ref, slab_ref, slab_sem, in_sem, kv_sem, stage_sem):
     rows, width = xf_ref.shape
-    ff = u_ref.shape[1]
+    ff = u_ref.shape[0] * 128
     text = kbuf.shape[1]
-    tn = ring_ref.shape[2]
+    tn = slab_ref.shape[1]
     per = tn // 128
     nt = width // tn
-    n_ff = ff // tn
-    k_parts = 1
-    while ff // k_parts > width or ff % k_parts:
-        k_parts += 1
-    kc = ff // k_parts
-    ring = Ring(ring_ref, ring_sem, [
-        (nt, cwq_ref, width, tn, 1, 0), (nt, cwo_ref, width, tn, 1, 0),
-        (n_ff, w1_ref, width, tn, 1, 0), (nt * k_parts, w2_ref, kc, tn, k_parts, 0)], 2)
+    n_k2 = ff // tn
+    blocks = -(-ff // width)
+    bc = ff // blocks
+    slabs = Slabs(slab_ref, slab_sem, [
+        (nt, cwq_ref, nt, width), (nt, cwo_ref, nt, width), (nt * blocks, w1_ref, nt, bc), (n_k2, w2_ref, n_k2, width)])
     x1_copy = pltpu.make_async_copy(x1_ref, xf_ref, in_sem)
     x1_copy.start()
-    ring.prime()
+    slabs.prime()
     load_vectors(vec_ref, (nw_ref, nb_ref, cgq_ref))
     NW, NB, CGQ = range(3)
     mod_ref[...] = te_ref[...] + bm_ref[...]
-    x1_copy.wait()
 
     def vec(n, k):
         return vec_ref[n, pl.ds(k, 1), :]
@@ -669,66 +727,84 @@
     def mod(n, k):
         return mod_ref[n, pl.ds(k, 1), :]
 
-    def dots(phase, n, lhs, finish):
-        def body(t, _):
-            slots = [ring.wait(phase, 2 * t + i) for i in range(2)]
-            for i in range(2):
-                finish(2 * t + i, dot(lhs[...], ring_ref[slots[i]]))
-            for i in range(2):
-                ring.refill(phase, 2 * t + i)
+    def clear(ref):
+        def body(j, _):
+            ref[:, cols_of(j, tn)] = jnp.zeros((rows, tn), F32)
             return 0
 
-        lax.fori_loop(0, n // 2, body, 0)
-
-    def norm_to(dst, mul, add, have_sum):
+        lax.fori_loop(0, nt, body, 0)
+
+    clear(h_ref)
+    x1_copy.wait()
+
+    def norm_to(dst, mul, add):
         def store(k, val):
-            dst[:, cols_of(k, 128)] = val.astype(BF16)
-
-        layer_norm(lambda k: xf_ref[:, cols_of(k, 128)], store, mul, add, rows, width, ss_ref, mean_ref, have_sum)
-
-    norm_to(b_ref, lambda k: vec(NW, k), lambda k: vec(NB, k), False)
-    ss_ref[...] = jnp.zeros_like(ss_ref)
-
-    def cq_done(i, acc):
-        h_ref[:, cols_of(i, tn)] = acc
-        add_lanes(ss_ref, rows, acc, True)
-
-    dots(0, nt, b_ref, cq_done)
-    rms_scale(ss_ref, rows, width)
-
-    def cq_head(j, _):
-        cols = cols_of(j, HEAD)
-        a_ref[:, cols] = ((h_ref[:, cols] * ss_ref[...]) * vec(CGQ, j)).astype(BF16)
-        return 0
-
+            dst[k] = val.astype(BF16)
+
+        layer_norm(lambda k: xf_ref[:, cols_of(k, 128)], store, mul, add, rows, width, ss_ref, mean_ref, False)
+
+    norm_to(b_ref, lambda k: vec(NW, k), lambda k: vec(NB, k))
+
+    def cq_slab(i, _):
+        slabs.add_product(0, i, b_ref, i, h_ref)
+        return 0
+
+    lax.fori_loop(0, nt, cq_slab, 0)
     gw = kbuf.shape[2]
     n_groups = width // gw
     heads = gw // HEAD
+    n_cva = cva_ref.shape[1] // gw
 
     def kv_loads(g, slot):
-        cols = cols_of(g, gw)
-        return (pltpu.make_async_copy(ck_ref.at[:, cols], kbuf.at[slot], kv_sem.at[0, slot]),
-                pltpu.make_async_copy(cv_ref.at[:, cols], vbuf.at[slot], kv_sem.at[1, slot]))
-
-    for c in kv_loads(0, 0):
-        c.start()
-    lax.fori_loop(0, width // HEAD, cq_head, 0)
+        return (pltpu.make_async_copy(ck_ref.at[:, cols_of(g, gw)], kbuf.at[slot], kv_sem.at[0, slot]),
+                pltpu.make_async_copy(cva_ref.at[:, cols_of(jnp.minimum(g, n_cva - 1), gw)], vbuf.at[slot], kv_sem.at[1, slot]),
+                pltpu.make_async_copy(cvb_ref.at[:, cols_of(jnp.maximum(g - n_cva, 0), gw)], vbuf.at[slot], kv_sem.at[1, slot]))
+
+    def kv_start(g, slot):
+        k_copy, va_copy, vb_copy = kv_loads(g, slot)
+        k_copy.start()
+
+        @pl.when(g < n_cva)
+        def _():
+            va_copy.start()
+
+        @pl.when(g >= n_cva)
+        def _():
+            vb_copy.start()
+
+    kv_start(jnp.int32(0), jnp.int32(0))
+    ss_ref[...] = jnp.zeros_like(ss_ref)
+
+    def cq_squares(i, _):
+        add_lanes(ss_ref, rows, h_ref[:, cols_of(i, tn)], True)
+        return 0
+
+    lax.fori_loop(0, nt, cq_squares, 0)
+    rms_scale(ss_ref, rows, width)
+
+    def cq_head(i, _):
+        for g in range(per):
+            k = i * per + g
+            a_ref[k] = ((h_ref[:, cols_of(k, 128)] * ss_ref[...]) * vec(CGQ, k)).astype(BF16)
+        return 0
+
+    lax.fori_loop(0, nt, cq_head, 0)
     s_refs = (s0_ref, s1_ref, s2_ref, s3_ref)
 
     def cross_group(g, _):
         slot = lax.rem(g, 2)
-        for c in kv_loads(g, slot):
-            c.wait()
+        k_copy, v_copy, _ = kv_loads(g, slot)
+        k_copy.wait()
+        v_copy.wait()
 
         @pl.when(g + 1 < n_groups)
         def _():
-            for c in kv_loads(g + 1, 1 - slot):
-                c.start()
+            kv_start(g + 1, 1 - slot)
 
         tops = []
 
         def score(j):
-            s = dot_nt(a_ref[:, cols_of(g * heads + j, HEAD)], kbuf[slot, :, j * HEAD:(j + 1) * HEAD])
+            s = dot_nt(a_ref[g * heads + j], kbuf[slot, :, j * HEAD:(j + 1) * HEAD])
             s_refs[j % 4][...] = s
             parts = groups(s)
             mx = parts[0]
@@ -744,7 +820,7 @@
                 total = total + p
                 parts.append(p.astype(BF16))
             acc = dot(jnp.concatenate(parts, axis=1), vbuf[slot, :, j * HEAD:(j + 1) * HEAD])
-            b_ref[:, cols_of(g * heads + j, HEAD)] = (acc / jnp.sum(total, axis=1, keepdims=True)).astype(BF16)
+            b_ref[g * heads + j] = (acc / jnp.sum(total, axis=1, keepdims=True)).astype(BF16)
 
         score(0)
         for j in range(1, heads):
@@ -754,94 +830,77 @@
         return 0
 
     lax.fori_loop(0, n_groups, cross_group, 0)
-    ss_ref[...] = jnp.zeros_like(ss_ref)
-
-    def co_done(i, acc):
-        total = ss_ref[...]
-        for g, a in enumerate(groups(acc)):
-            cols = cols_of(i * per + g, 128)
-            x2 = xf_ref[:, cols] + a
-            xf_ref[:, cols] = x2
-            total = total + x2
-        ss_ref[...] = total
-
-    dots(1, nt, b_ref, co_done)
-    norm_to(a_ref, lambda k: 1.0 + mod(SC2, k), lambda k: mod(SH2, k), True)
-
-    def f1_gelu(i, src, g):
-        u_ref[:, cols_of(i * per + g, 128)] = jax.nn.gelu(src[:, g * 128:(g + 1) * 128], approximate=True).astype(BF16)
-
-    def f1_dot(slot, dst, old, src):
-        acc = None
-        kp = width // per
-        for g in range(per):
-            term = dot(a_ref[:, g * kp:(g + 1) * kp], ring_ref[slot, g * kp:(g + 1) * kp, :])
-            acc = term if acc is None else acc + term
-            if src is not None:
-                f1_gelu(old, src, g)
-        dst[...] = acc
-
-    f1_dot(ring.wait(2, 0), g0_ref, None, None)
-    ring.refill(2, 0)
-
-    def f1_pair(t, _):
-        i = 2 * t + 1
-        slots = [ring.wait(2, i), ring.wait(2, i + 1)]
-        f1_dot(slots[0], g1_ref, i - 1, g0_ref)
-        f1_dot(slots[1], g0_ref, i, g1_ref)
-        ring.refill(2, i)
-        ring.refill(2, i + 1)
-        return 0
-
-    lax.fori_loop(0, (n_ff - 1) // 2, f1_pair, 0)
-    for g in range(per):
-        f1_gelu(n_ff - 1, g0_ref, g)
+
+    def co_slab(i, _):
+        slabs.add_product(1, i, b_ref, i, xf_ref)
+        return 0
+
+    lax.fori_loop(0, nt, co_slab, 0)
+    norm_to(a_ref, lambda k: 1.0 + mod(SC2, k), lambda k: mod(SH2, k))
+
+    def f1_block(c, _):
+        clear(h_ref)
+
+        def f1_slab(k, _):
+            slabs.add_product(2, c * nt + k, a_ref, k, h_ref)
+            return 0
+
+        lax.fori_loop(0, nt, f1_slab, 0)
+
+        def gelu(j, _):
+            u_ref[c * (bc // 128) + j] = jax.nn.gelu(h_ref[:, cols_of(j, 128)], approximate=True).astype(BF16)
+            return 0
+
+        lax.fori_loop(0, bc // 128, gelu, 0)
+        return 0
+
+    lax.fori_loop(0, blocks, f1_block, 0)
+    clear(h_ref)
+
+    def f2_slab(k, _):
+        slabs.add_product(3, k, u_ref, k, h_ref)
+        return 0
+
+    lax.fori_loop(0, n_k2, f2_slab, 0)
 
     def stage_copy(i, slot):
         return pltpu.make_async_copy(stage_ref.at[slot], out_ref.at[:, cols_of(i, tn)], stage_sem.at[slot])
 
-    def f2_tile(i, _):
+    def finish(i, _):
         s = lax.rem(i, 2)
-        slots = [ring.wait(3, i * k_parts + c) for c in range(k_parts)]
 
         @pl.when(i >= 2)
         def _():
             stage_copy(i, s).wait()
 
-        acc = None
-        for c in range(k_parts):
-            term = dot(u_ref[:, c * kc:(c + 1) * kc], ring_ref[slots[c], 0:kc, :])
-            acc = term if acc is None else acc + term
-        for g, a in enumerate(groups(acc)):
+        for g in range(per):
             k = i * per + g
-            stage_ref[s, :, g * 128:(g + 1) * 128] = (xf_ref[:, cols_of(k, 128)] + mod(G2, k) * a).astype(BF16)
+            stage_ref[s, :, g * 128:(g + 1) * 128] = (xf_ref[:, cols_of(k, 128)] + mod(G2, k) * h_ref[:, cols_of(k, 128)]).astype(BF16)
         stage_copy(i, s).start()
-        for c in range(k_parts):
-            ring.refill(3, i * k_parts + c)
-        return 0
-
-    lax.fori_loop(0, nt, f2_tile, 0)
+        return 0
+
+    lax.fori_loop(0, nt, finish, 0)
     for i in range(2):
         stage_copy(0, i).wait()
 
 
-def tail_call(te, bm, vectors, x1, ck, cv, cwq, cwo, w1, w2, tn):
+def tail_call(te, bm, vectors, x1, ck, cva, cvb, cwq, cwo, w1, w2, tn):
     rows, width = x1.shape
     text = ck.shape[0]
     ff = w1.shape[1]
+    depth = 4
     flops = 2 * rows * width * (2 * width + 2 * ff) + 4 * rows * text * width
-    assert (width // tn) % 2 == 0 and (ff // tn) % 2 == 1 and len(vectors) == 3
     return pl.pallas_call(
         tail_kernel,
         out_shape=jax.ShapeDtypeStruct((rows, width), BF16),
-        in_specs=[vmem_spec()] * (2 + len(vectors)) + [any_spec()] * 7,
+        in_specs=[vmem_spec()] * (2 + len(vectors)) + [any_spec()] * 8,
         out_specs=any_spec(),
         scratch_shapes=[
-            pltpu.VMEM((rows, width), BF16),
-            pltpu.VMEM((rows, width), BF16),
+            pltpu.VMEM((width // 128, rows, 128), BF16),
+            pltpu.VMEM((width // 128, rows, 128), BF16),
             pltpu.VMEM((rows, width), F32),
             pltpu.VMEM((rows, width), F32),
-            pltpu.VMEM((rows, ff), BF16),
+            pltpu.VMEM((ff // 128, rows, 128), BF16),
             pltpu.VMEM((rows, 128), F32),
             pltpu.VMEM((rows, 128), F32),
             pltpu.VMEM((len(vectors), width // 128, 128), F32),
@@ -852,11 +911,9 @@
             pltpu.VMEM((rows, text), F32),
             pltpu.VMEM((rows, text), F32),
             pltpu.VMEM((rows, text), F32),
-            pltpu.VMEM((rows, tn), F32),
-            pltpu.VMEM((rows, tn), F32),
             pltpu.VMEM((2, rows, tn), BF16),
-            pltpu.VMEM((5, width, tn), BF16),
-            pltpu.SemaphoreType.DMA((5,)),
+            pltpu.VMEM((depth, tn, width), BF16),
+            pltpu.SemaphoreType.DMA((depth,)),
             pltpu.SemaphoreType.DMA,
             pltpu.SemaphoreType.DMA((2, 2)),
             pltpu.SemaphoreType.DMA((2,)),
@@ -864,7 +921,7 @@
         compiler_params=pltpu.CompilerParams(vmem_limit_bytes=VMEM_LIMIT),
         cost_estimate=pl.CostEstimate(flops=flops, bytes_accessed=2 * width * (2 * width + 2 * ff), transcendentals=rows * ff),
         name='tail',
-    )(te, bm, *vectors, x1, ck, cv, cwq, cwo, w1, w2)
+    )(te, bm, *vectors, x1, ck, cva, cvb, cwq, cwo, w1, w2)
 
 
 def solution(mesh):
@@ -879,10 +936,12 @@
         def lanes(*vectors):
             return tuple(v.reshape(-1, 128) for v in vectors)
 
-        q, k, v, ck = qkv_call(x, te, bm, rope_ang, lanes(attn_bq, attn_bk, attn_bv, attn_gq, attn_gk, cross_gk), ctx,
-                               attn_wv, attn_wk, attn_wq, cross_wk, tn)
-        x1, cv = attend_call(te, bm, *lanes(attn_bo), q, k, v, ctx, cross_wv, x, attn_wo, tn)
-        out = tail_call(te, bm, lanes(norm3_w, norm3_b, cross_gq), x1, ck, cv, cross_wq, cross_wo, ffn_w1, ffn_w2, tn)
+        cv_a = max(1024, x.shape[1] * 2 // 5 // 1024 * 1024)
+        cv_b = x.shape[1] - cv_a
+        q, k, v, ck, cva = qkv_call(x, te, bm, rope_ang, lanes(attn_bq, attn_bk, attn_bv, attn_gq, attn_gk, cross_gk), ctx,
+                                    attn_wv, attn_wk, attn_wq, cross_wk, cross_wv, cv_a, tn)
+        x1, cvb = attend_call(te, bm, *lanes(attn_bo), q, k, v, ctx, cross_wv, x, attn_wo, cv_b, tn)
+        out = tail_call(te, bm, lanes(norm3_w, norm3_b, cross_gq), x1, ck, cva, cvb, cross_wq, cross_wo, ffn_w1, ffn_w2, tn)
         return out[None]
 
     in_specs = (tok_spec, P(('sp', 'uly'), None), batch_spec, P(), batch_spec) + (P(),) * 20

time: 472 us -> 457 us (0.968)
  Pallas kernels: 469 us -> 455 us
    pallas_call x1, Pallas kernels: 184 us -> 171 us  [tail_call(): pl.pallas_call(tail_kernel, out_shape=jax.ShapeDtypeStruct((rows, width),...]
where the time goes in v4:
time: 457 us; the launch traced here: 456 us
  Pallas kernels  455 us (100%)
    pallas_call x1, Pallas kernels, tail_call(): pl.pallas_call(tail_kernel, out_shape=jax.ShapeDtypeStruct((rows, width),...  171 us
    pallas_call x1, Pallas kernels, attend_call(): pl.pallas_call(attend_kernel, out_shape=(jax.ShapeDtypeStruct((rows, widt...  145 us
    pallas_call x1, Pallas kernels, qkv_call(): pl.pallas_call(qkv_kernel, out_shape=(split, gathered, gathered, jax.Shap...  139 us

profile of v4, /device:TPU:8, one launch (start us, length us, event | category | flops | bytes accessed | tf_op | source)
XLA Modules:
  0.0 456.4 jit_solution(12814140386170132597)
XLA Ops:
  0.0 1.7 copy.26.ang_ref
  1.7 139.2 %qkv.1 = (bf16[8,288,640]{2,1,0:T(8,128)(2,1)}, bf16[2304,640]{1,0:T(8,128)(2,1)}, bf16[2304,640]{1,0:T(8,128)(2,1)}, bf16[512,5120]{1,0:T(8,128)(2,1)}, bf16[512,2048]{1,0:T(8,128)(2,1)}) custom-call(bf16[288,5120]{1,0:T(8,128)(2,1)} %bitcast.17, f32[6,40,128]{2,1,0:T(8,128)} %bitcast.19, f32[6,40,128]{2,1,0:T(8,128)} %bitcast.22, f32[288,64]{1,0:T(8,128)} %copy.26.ang_ref, ...), custom_call_target="tpu_custom_call" | custom-call | flops 82879447040 | bytes 209715200 | tf_op jit(solution)/shard_map/qkv/pallas_call | solution.py:358
  140.8 144.7 %attend.1 = (f32[288,5120]{1,0:T(8,128)}, bf16[512,3072]{1,0:T(8,128)(2,1)}) custom-call(f32[6,40,128]{2,1,0:T(8,128)} %bitcast.20, f32[6,40,128]{2,1,0:T(8,128)} %bitcast.23, bf16[40,128]{1,0:T(8,128)(2,1)} %bitcast.31, bf16[8,288,640]{2,1,0:T(8,128)(2,1)} %get-tuple-element.12.q_ref, bf16[2304,640]{1,0:T(8,128)(2,1)} %get-tuple-element.13.k_ref, ...), custom_call_target="tpu_custom_call" | custom-call | flops 58384711680 | bytes 116654080 | tf_op jit(solution)/shard_map/attend/pallas_call | solution.py:619
  285.6 170.7 %tail.1 = bf16[288,5120]{1,0:T(8,128)(2,1)} custom-call(f32[6,40,128]{2,1,0:T(8,128)} %bitcast.21, f32[6,40,128]{2,1,0:T(8,128)} %bitcast.24, bf16[40,128]{1,0:T(8,128)(2,1)} %bitcast.32, bf16[40,128]{1,0:T(8,128)(2,1)} %bitcast.33, bf16[40,128]{1,0:T(8,128)(2,1)} %bitcast.34, f32[288,5120]{1,0:T(8,128)} %get-tuple-element.15.x1_ref, ...), custom_call_target="tpu_custom_call" | custom-call | flops 114756157440 | bytes 387973120 | tf_op jit(solution)/shard_map/tail/pallas_call | solution.py:893

commit v5 on v4

--- a/solution.py
+++ b/solution.py
@@ -10,6 +10,7 @@
 EPS = 1e-6
 HEAD = 128
 LOG2E = 1.4426950408889634
+GELU_A = 0.7978845608028654
 SM_C = (HEAD ** -0.5) * LOG2E
 MESH = pl.DeviceIdType.MESH
 CHIPS = 8
@@ -26,6 +27,11 @@
 
 def dot_nt(a, b):
     return lax.dot_general(a, b, (((1,), (1,)), ((), ())), preferred_element_type=F32)
+
+
+def gelu_tanh(x):
+    half = 0.5 * x
+    return half + half * jnp.tanh(x * (GELU_A + (GELU_A * 0.044715) * (x * x)))
 
 
 def my_place():
@@ -218,12 +224,25 @@
     def q_copies():
         return [pltpu.make_async_copy(qkv_ref.at[2, :, pl.ds(d * part, part)], q_out.at[d], out_sem.at[2]) for d in range(CHIPS)]
 
+    def far_pieces(t):
+        out = []
+        for j in range(CHIPS // 2):
+            lo, hi = max(t * tn, j * part), min((t + 1) * tn, (j + 1) * part)
+            if lo < hi:
+                src = pl.ds(pl.multiple_of(far * part + lo, 128), hi - lo)
+                r = flip(me, far + j)
+                out.append(pltpu.make_async_remote_copy(
+                    src_ref=qkv_ref.at[0, :, src], dst_ref=v_out.at[cols_of(me, rows), pl.ds(lo - j * part, hi - lo)],
+                    send_sem=send_sem.at[0, r], recv_sem=recv_sem.at[0, r], device_id=device_at(far + j, core), device_id_type=MESH))
+        return out
+
     def v_tile(i, _):
         slot = ring.wait(0, i)
-        for j in range(CHIPS // 2):
-            @pl.when(i == -(-part * (j + 1) // tn))
+        for t in range(nt // 2):
+            @pl.when(i == t + 1)
             def _():
-                remote(0, v_out, flip(me, far + j)).start()
+                for c in far_pieces(t):
+                    c.start()
 
         ct = lax.rem(i + shift, nt)
         for g, a in enumerate(groups(dot(y_ref[...], ring_ref[slot]))):
@@ -238,11 +257,14 @@
         for r in range(1, CHIPS // 2):
             remote(0, v_out, r).start()
         local(0, v_out).start()
-        lane = lax.broadcasted_iota(jnp.int32, (rows, HEAD), 1)
-        ang = jnp.concatenate([ang_ref[...], ang_ref[...]], axis=1)
-        spread = jnp.take_along_axis(ang, lane // 2, axis=1)
-        cos_ref[...] = jnp.cos(spread)
-        sin_ref[...] = jnp.where(lax.rem(lane, 2) == 0, -1.0, 1.0) * jnp.sin(spread)
+        pick = (lax.broadcasted_iota(jnp.int32, (HEAD // 2, HEAD), 1) // 2 == lax.broadcasted_iota(jnp.int32, (HEAD // 2, HEAD), 0)).astype(F32)
+        sign = 2.0 * lax.rem(lax.broadcasted_iota(jnp.int32, (HEAD // 2, HEAD), 1), 2).astype(F32) - 1.0
+
+        def spread(table, picker):
+            return lax.dot_general(table, picker, (((0,), (0,)), ((), ())), precision=lax.Precision.HIGHEST, preferred_element_type=F32)
+
+        cos_ref[...] = spread(jnp.cos(ang_ref[...]), pick)
+        sin_ref[...] = spread(jnp.sin(ang_ref[...]), pick * sign)
 
     def k_all():
         for r in range(CHIPS - 1, 0, -1):
@@ -386,9 +408,9 @@
     )(x, te, bm, ang, *vectors, ctx, wv, wk, wq, cwk, cwv)
 
 
-def attend_kernel(te_ref, bm_ref, bo_ref, q_ref, k_ref, v_ref, ctx_hbm, cwv_ref, x_hbm, wo_ref, x1_out, cv_out,
+def attend_kernel(te_ref, bm_ref, bo_ref, q_ref, k_ref, v_ref, ctx_hbm, cwv_ref, x_hbm, wo_ref, x1_out, sum_out, cv_out,
                   kbuf, vbuf, qbuf, obuf, s0_ref, s1_ref, mx0_ref, mx1_ref, ctx_ref, stage_ref, ring_ref, acc_ref, wo_ring, row_ref,
-                  own_sem, pair_send, pair_recv, q_send, q_recv, o_send, o_recv, ctx_sem, stage_sem, ring_sem, wo_sem):
+                  own_sem, pair_send, pair_recv, q_send, q_recv, o_send, o_recv, ctx_sem, stage_sem, ring_sem, wo_sem, x_sem):
     n_heads, keys, _ = kbuf.shape
     half = keys // 2
     rows = qbuf.shape[1]
@@ -551,8 +573,10 @@
     row_ref[0] = te_ref[G1] + bm_ref[G1]
     row_ref[1] = bo_ref[...].astype(F32)
 
-    def project(r, lhs, side, finish):
+    def project(r, lhs, side, finish, ready=None):
         wo_copy(r, side).wait()
+        if ready is not None:
+            ready()
         for n in range(half_n // tn):
             cols = pl.ds(side * half_n + n * tn, tn)
             finish(cols, side * half_n + n * tn, dot(lhs[...], wo_ring[side, :, n * tn:(n + 1) * tn]))
@@ -564,10 +588,14 @@
         acc_ref[:, cols] = acc_ref[:, cols] + prod
 
     def last(cols, c0, prod):
+        total = mx0_ref[...]
         for g, p in enumerate(groups(prod)):
             k = c0 // 128 + g
             gc = slice(c0 + g * 128, c0 + (g + 1) * 128)
-            acc_ref[:, gc] = ctx_ref[0:rows, gc].astype(F32) + row_ref[0, k:k + 1, :] * (acc_ref[:, gc] + p + row_ref[1, k:k + 1, :])
+            x1 = ctx_ref[0:rows, gc].astype(F32) + row_ref[0, k:k + 1, :] * (acc_ref[:, gc] + p + row_ref[1, k:k + 1, :])
+            acc_ref[:, gc] = x1
+            total = total + x1
+        mx0_ref[...] = total
 
     def arrived(r):
         for h in range(n_heads):
@@ -591,9 +619,9 @@
     lax.fori_loop(1, CHIPS - 1, chunk, 0)
     x_copy.wait()
     arrived(CHIPS - 1)
+    mx0_ref[...] = jnp.zeros_like(mx0_ref)
     project(CHIPS - 1, obuf.at[CHIPS - 1], 0, last)
-    project(CHIPS - 1, obuf.at[CHIPS - 1], 1, last)
-    x1_copy(0).start()
+    project(CHIPS - 1, obuf.at[CHIPS - 1], 1, last, lambda: x1_copy(0).start())
     for h in range(n_heads):
         for c in pair(h):
             c.wait_send()
@@ -606,8 +634,11 @@
 
     lax.fori_loop(1, CHIPS, drain, 0)
     x1_copy(1).start()
+    sum_copy = pltpu.make_async_copy(mx0_ref, sum_out, x_sem)
+    sum_copy.start()
     for side in range(2):
         x1_copy(side).wait()
+    sum_copy.wait()
 
 
 def attend_call(te, bm, bo, q, k, v, ctx, cwv, x, wo, cv_cols, tn):
@@ -618,9 +649,9 @@
     flops = 8 * half * half * part + 2 * width * (text * cv_cols + rows * width)
     return pl.pallas_call(
         attend_kernel,
-        out_shape=(jax.ShapeDtypeStruct((rows, width), F32), jax.ShapeDtypeStruct((text, cv_cols), BF16)),
+        out_shape=(jax.ShapeDtypeStruct((rows, width), F32), jax.ShapeDtypeStruct((rows, 128), F32), jax.ShapeDtypeStruct((text, cv_cols), BF16)),
         in_specs=[vmem_spec()] * 3 + [any_spec()] * 7,
-        out_specs=[any_spec()] * 2,
+        out_specs=[any_spec()] * 3,
         scratch_shapes=[
             pltpu.VMEM((n_heads, 2 * half, HEAD), BF16),
             pltpu.VMEM((n_heads, 2 * half, HEAD), BF16),
@@ -647,6 +678,7 @@
             pltpu.SemaphoreType.DMA((2,)),
             pltpu.SemaphoreType.DMA((2,)),
             pltpu.SemaphoreType.DMA((2,)),
+            pltpu.SemaphoreType.DMA,
         ],
         compiler_params=pltpu.CompilerParams(vmem_limit_bytes=VMEM_LIMIT, collective_id=1, has_side_effects=True),
         cost_estimate=pl.CostEstimate(flops=flops, bytes_accessed=8 * half * part + 4 * width * width, transcendentals=2 * half * half * n_heads),
@@ -676,33 +708,46 @@
         for i in range(self.depth):
             self.start(0, i)
 
-    def add_product(self, phase, i, lhs, k, acc_ref):
+    def add_product(self, phase, i, m, lhs, k, acc_ref, fresh=False, finish=None):
         n, _, _, n_cols = self.phases[phase]
-        for c in self.copies(phase, i):
-            c.wait()
-        slot = lax.rem(self.base[phase] + i, self.depth)
+        for j in range(m):
+            for c in self.copies(phase, i + j):
+                c.wait()
+        slots = [lax.rem(self.base[phase] + i + j, self.depth) for j in range(m)]
         per = self.rows // 128
-        left = jnp.concatenate([lhs[k * per + g] for g in range(per)], axis=1)
+        left = [jnp.concatenate([lhs[(k + j) * per + g] for g in range(per)], axis=1) for j in range(m)]
         c0 = 0
+        waiting = None
         while c0 < n_cols:
             cols = slice(c0, min(c0 + 512, n_cols))
-            acc_ref[:, cols] = acc_ref[:, cols] + dot(left, self.slots[slot, :, cols])
+            total = dot(left[0], self.slots[slots[0], :, cols])
+            for j in range(1, m):
+                total = total + dot(left[j], self.slots[slots[j], :, cols])
+            old = acc_ref[:, cols]
+            acc_ref[:, cols] = total + (jnp.where(k > 0, old, 0.0) if fresh else old)
+            if finish is not None:
+                if waiting is not None:
+                    finish(waiting)
+                waiting = cols
             c0 += 512
-        ahead = i + self.depth
-
-        @pl.when(ahead < n)
-        def _():
-            self.start(phase, ahead)
-
-        if phase + 1 < len(self.phases):
-            @pl.when(ahead >= n)
+        if waiting is not None:
+            finish(waiting)
+        for j in range(m):
+            ahead = i + j + self.depth
+
+            @pl.when(ahead < n)
             def _():
-                self.start(phase + 1, ahead - n)
-
-
-def tail_kernel(te_ref, bm_ref, nw_ref, nb_ref, cgq_ref, x1_ref, ck_ref, cva_ref, cvb_ref, cwq_ref, cwo_ref, w1_ref, w2_ref,
+                self.start(phase, ahead)
+
+            if phase + 1 < len(self.phases):
+                @pl.when(ahead >= n)
+                def _():
+                    self.start(phase + 1, ahead - n)
+
+
+def tail_kernel(te_ref, bm_ref, nw_ref, nb_ref, cgq_ref, x1_ref, sum_ref, ck_ref, cva_ref, cvb_ref, cwq_ref, cwo_ref, w1_ref, w2_ref,
                 out_ref, a_ref, b_ref, xf_ref, h_ref, u_ref, ss_ref, mean_ref, vec_ref, mod_ref, kbuf, vbuf,
-                s0_ref, s1_ref, s2_ref, s3_ref, stage_ref, slab_ref, slab_sem, in_sem, kv_sem, stage_sem):
+                s0_ref, s1_ref, s2_ref, s3_ref, stage_ref, slab_ref, slab_sem, in_sem, sum_sem, kv_sem, stage_sem):
     rows, width = xf_ref.shape
     ff = u_ref.shape[0] * 128
     text = kbuf.shape[1]
@@ -716,6 +761,8 @@
         (nt, cwq_ref, nt, width), (nt, cwo_ref, nt, width), (nt * blocks, w1_ref, nt, bc), (n_k2, w2_ref, n_k2, width)])
     x1_copy = pltpu.make_async_copy(x1_ref, xf_ref, in_sem)
     x1_copy.start()
+    sum_copy = pltpu.make_async_copy(sum_ref, ss_ref, sum_sem)
+    sum_copy.start()
     slabs.prime()
     load_vectors(vec_ref, (nw_ref, nb_ref, cgq_ref))
     NW, NB, CGQ = range(3)
@@ -727,26 +774,19 @@
     def mod(n, k):
         return mod_ref[n, pl.ds(k, 1), :]
 
-    def clear(ref):
-        def body(j, _):
-            ref[:, cols_of(j, tn)] = jnp.zeros((rows, tn), F32)
-            return 0
-
-        lax.fori_loop(0, nt, body, 0)
-
-    clear(h_ref)
     x1_copy.wait()
-
-    def norm_to(dst, mul, add):
+    sum_copy.wait()
+
+    def norm_to(dst, mul, add, have_sum):
         def store(k, val):
             dst[k] = val.astype(BF16)
 
-        layer_norm(lambda k: xf_ref[:, cols_of(k, 128)], store, mul, add, rows, width, ss_ref, mean_ref, False)
-
-    norm_to(b_ref, lambda k: vec(NW, k), lambda k: vec(NB, k))
+        layer_norm(lambda k: xf_ref[:, cols_of(k, 128)], store, mul, add, rows, width, ss_ref, mean_ref, have_sum)
+
+    norm_to(b_ref, lambda k: vec(NW, k), lambda k: vec(NB, k), True)
 
     def cq_slab(i, _):
-        slabs.add_product(0, i, b_ref, i, h_ref)
+        slabs.add_product(0, i, 1, b_ref, i, h_ref, True)
         return 0
 
     lax.fori_loop(0, nt, cq_slab, 0)
@@ -832,36 +872,35 @@
     lax.fori_loop(0, n_groups, cross_group, 0)
 
     def co_slab(i, _):
-        slabs.add_product(1, i, b_ref, i, xf_ref)
+        slabs.add_product(1, i, 1, b_ref, i, xf_ref)
         return 0
 
     lax.fori_loop(0, nt, co_slab, 0)
-    norm_to(a_ref, lambda k: 1.0 + mod(SC2, k), lambda k: mod(SH2, k))
+    norm_to(a_ref, lambda k: 1.0 + mod(SC2, k), lambda k: mod(SH2, k), False)
 
     def f1_block(c, _):
-        clear(h_ref)
-
-        def f1_slab(k, _):
-            slabs.add_product(2, c * nt + k, a_ref, k, h_ref)
+        def f1_pair(t, _):
+            slabs.add_product(2, c * nt + 2 * t, 2, a_ref, 2 * t, h_ref, True)
             return 0
 
-        lax.fori_loop(0, nt, f1_slab, 0)
-
-        def gelu(j, _):
-            u_ref[c * (bc // 128) + j] = jax.nn.gelu(h_ref[:, cols_of(j, 128)], approximate=True).astype(BF16)
-            return 0
-
-        lax.fori_loop(0, bc // 128, gelu, 0)
+        lax.fori_loop(0, nt // 2 - 1, f1_pair, 0)
+
+        def gelu(cols):
+            for g, x in enumerate(groups(h_ref[:, cols])):
+                u_ref[c * (bc // 128) + cols.start // 128 + g] = gelu_tanh(x).astype(BF16)
+
+        slabs.add_product(2, c * nt + nt - 2, 2, a_ref, nt - 2, h_ref, False, gelu)
         return 0
 
     lax.fori_loop(0, blocks, f1_block, 0)
-    clear(h_ref)
-
-    def f2_slab(k, _):
-        slabs.add_product(3, k, u_ref, k, h_ref)
-        return 0
-
-    lax.fori_loop(0, n_k2, f2_slab, 0)
+
+    def f2_pair(t, _):
+        slabs.add_product(3, 2 * t, 2, u_ref, 2 * t, h_ref, True)
+        return 0
+
+    lax.fori_loop(0, n_k2 // 2, f2_pair, 0)
+    if n_k2 % 2:
+        slabs.add_product(3, n_k2 - 1, 1, u_ref, n_k2 - 1, h_ref)
 
     def stage_copy(i, slot):
         return pltpu.make_async_copy(stage_ref.at[slot], out_ref.at[:, cols_of(i, tn)], stage_sem.at[slot])
@@ -884,16 +923,16 @@
         stage_copy(0, i).wait()
 
 
-def tail_call(te, bm, vectors, x1, ck, cva, cvb, cwq, cwo, w1, w2, tn):
+def tail_call(te, bm, vectors, x1, sums, ck, cva, cvb, cwq, cwo, w1, w2, tn):
     rows, width = x1.shape
     text = ck.shape[0]
     ff = w1.shape[1]
-    depth = 4
+    depth = 5
     flops = 2 * rows * width * (2 * width + 2 * ff) + 4 * rows * text * width
     return pl.pallas_call(
         tail_kernel,
         out_shape=jax.ShapeDtypeStruct((rows, width), BF16),
-        in_specs=[vmem_spec()] * (2 + len(vectors)) + [any_spec()] * 8,
+        in_specs=[vmem_spec()] * (2 + len(vectors)) + [any_spec()] * 9,
         out_specs=any_spec(),
         scratch_shapes=[
             pltpu.VMEM((width // 128, rows, 128), BF16),
@@ -915,13 +954,14 @@
             pltpu.VMEM((depth, tn, width), BF16),
             pltpu.SemaphoreType.DMA((depth,)),
             pltpu.SemaphoreType.DMA,
+            pltpu.SemaphoreType.DMA,
             pltpu.SemaphoreType.DMA((2, 2)),
             pltpu.SemaphoreType.DMA((2,)),
         ],
         compiler_params=pltpu.CompilerParams(vmem_limit_bytes=VMEM_LIMIT),
         cost_estimate=pl.CostEstimate(flops=flops, bytes_accessed=2 * width * (2 * width + 2 * ff), transcendentals=rows * ff),
         name='tail',
-    )(te, bm, *vectors, x1, ck, cva, cvb, cwq, cwo, w1, w2)
+    )(te, bm, *vectors, x1, sums, ck, cva, cvb, cwq, cwo, w1, w2)
 
 
 def solution(mesh):
@@ -938,10 +978,10 @@
 
         cv_a = max(1024, x.shape[1] * 2 // 5 // 1024 * 1024)
         cv_b = x.shape[1] - cv_a
-        q, k, v, ck, cva = qkv_call(x, te, bm, rope_ang, lanes(attn_bq, attn_bk, attn_bv, attn_gq, attn_gk, cross_gk), ctx,
+        q, k, v, ck, cva = qkv_call(x, te, bm, rope_ang.T, lanes(attn_bq, attn_bk, attn_bv, attn_gq, attn_gk, cross_gk), ctx,
                                     attn_wv, attn_wk, attn_wq, cross_wk, cross_wv, cv_a, tn)
-        x1, cvb = attend_call(te, bm, *lanes(attn_bo), q, k, v, ctx, cross_wv, x, attn_wo, cv_b, tn)
-        out = tail_call(te, bm, lanes(norm3_w, norm3_b, cross_gq), x1, ck, cva, cvb, cross_wq, cross_wo, ffn_w1, ffn_w2, tn)
+        x1, sums, cvb = attend_call(te, bm, *lanes(attn_bo), q, k, v, ctx, cross_wv, x, attn_wo, cv_b, tn)
+        out = tail_call(te, bm, lanes(norm3_w, norm3_b, cross_gq), x1, sums, ck, cva, cvb, cross_wq, cross_wo, ffn_w1, ffn_w2, tn)
         return out[None]
 
     in_specs = (tok_spec, P(('sp', 'uly'), None), batch_spec, P(), batch_spec) + (P(),) * 20

time: 457 us -> 444 us (0.972)
  Pallas kernels: 455 us -> 444 us
    pallas_call x1, Pallas kernels: 171 us -> 163 us  [tail_call(): pl.pallas_call(tail_kernel, out_shape=jax.ShapeDtypeStruct((rows, width),...]
where the time goes in v5:
time: 444 us
  Pallas kernels  444 us (100%)
    pallas_call x1, Pallas kernels, tail_call(): pl.pallas_call(tail_kernel, out_shape=jax.ShapeDtypeStruct((rows, width),...  163 us
    pallas_call x1, Pallas kernels, attend_call(): pl.pallas_call(attend_kernel, out_shape=(jax.ShapeDtypeStruct((rows, widt...  144 us
    pallas_call x1, Pallas kernels, qkv_call(): pl.pallas_call(qkv_kernel, out_shape=(split, gathered, gathered, jax.Shap...  137 us

profile of v5, /device:TPU:8, one launch (start us, length us, event | category | flops | bytes accessed | tf_op | source)
XLA Modules:
  0.0 443.9 jit_solution(13294501952190419905)
XLA Ops:
  0.0 137.4 %qkv.1 = (bf16[8,288,640]{2,1,0:T(8,128)(2,1)}, bf16[2304,640]{1,0:T(8,128)(2,1)}, bf16[2304,640]{1,0:T(8,128)(2,1)}, bf16[512,5120]{1,0:T(8,128)(2,1)}, bf16[512,2048]{1,0:T(8,128)(2,1)}) custom-call(bf16[288,5120]{1,0:T(8,128)(2,1)} %bitcast.18, f32[6,40,128]{2,1,0:T(8,128)} %bitcast.20, f32[6,40,128]{2,1,0:T(8,128)} %bitcast.23, f32[64,288]{1,0:T(8,128)} %bitcast.26, ...), custom_call_target="tpu_custom_call" | custom-call | flops 82879447040 | bytes 209715200 | tf_op jit(solution)/shard_map/qkv/pallas_call | solution.py:380
  137.4 143.6 %attend.1 = (f32[288,5120]{1,0:T(8,128)}, f32[288,128]{1,0:T(8,128)}, bf16[512,3072]{1,0:T(8,128)(2,1)}) custom-call(f32[6,40,128]{2,1,0:T(8,128)} %bitcast.21, f32[6,40,128]{2,1,0:T(8,128)} %bitcast.24, bf16[40,128]{1,0:T(8,128)(2,1)} %bitcast.33, bf16[8,288,640]{2,1,0:T(8,128)(2,1)} %get-tuple-element.13.q_ref, bf16[2304,640]{1,0:T(8,128)(2,1)} %get-tuple-element.14.k_ref, ...), custom_call_target="tpu_custom_call" | custom-call | flops 58384711680 | bytes 116654080 | tf_op jit(solution)/shard_map/attend/pallas_call | solution.py:650
  281.1 162.6 %tail.1 = bf16[288,5120]{1,0:T(8,128)(2,1)} custom-call(f32[6,40,128]{2,1,0:T(8,128)} %bitcast.22, f32[6,40,128]{2,1,0:T(8,128)} %bitcast.25, bf16[40,128]{1,0:T(8,128)(2,1)} %bitcast.34, bf16[40,128]{1,0:T(8,128)(2,1)} %bitcast.35, bf16[40,128]{1,0:T(8,128)(2,1)} %bitcast.36, f32[288,5120]{1,0:T(8,128)} %get-tuple-element.16.x1_ref, ...), custom_call_target="tpu_custom_call" | custom-call | flops 114756157440 | bytes 387973120 | tf_op jit(solution)/shard_map/tail/pallas_call | solution.py:932
